TPU v7x, 8 devices: a whole 2x2x1 slice. The times are simulated.
8 devices in a mesh: dp: 1 (over z), kv: 2 (over y), tp: 4 (over x, core).
Axes of the slice: x: 2, y: 2, z: 1, core: 2. Of those that a mesh axis runs over, the one named last changes fastest.
Arguments:
- x: bfloat16 [64, 2048], P('dp')
- ks_cache: bfloat16 [64, 8, 1024, 64], P('dp', 'tp', 'kv')
- vs_cache: bfloat16 [64, 8, 1024, 64], P('dp', 'tp', 'kv')
- seq_len: int32 [64], P('dp')
- kx_cache: bfloat16 [64, 8, 6404, 64], P('dp', 'tp', 'kv')
- vx_cache: bfloat16 [64, 8, 6404, 64], P('dp', 'tp', 'kv')
- tile_vis: int32 [64, 4], P('dp')
- attn_norm: bfloat16 [2048], replicated
- wq_self: bfloat16 [2048, 2048], P(None, 'tp')
- wk_self: bfloat16 [2048, 512], P(None, 'tp')
- wv_self: bfloat16 [2048, 512], P(None, 'tp')
- wo_self: bfloat16 [2048, 2048], P('tp')
- mlp_norm: bfloat16 [2048], replicated
- wg_self: bfloat16 [2048, 8192], P(None, 'tp')
- wu_self: bfloat16 [2048, 8192], P(None, 'tp')
- wd_self: bfloat16 [8192, 2048], P('tp')
- xattn_norm: bfloat16 [2048], replicated
- wq_cross: bfloat16 [2048, 2048], P(None, 'tp')
- q_norm: bfloat16 [64], replicated
- wo_cross: bfloat16 [2048, 2048], P('tp')
- cross_gates: float32 [2], replicated
- xmlp_norm: bfloat16 [2048], replicated
- wg_cross: bfloat16 [2048, 8192], P(None, 'tp')
- wu_cross: bfloat16 [2048, 8192], P(None, 'tp')
- wd_cross: bfloat16 [8192, 2048], P('tp')
Outputs:
- output 1: bfloat16 [64, 2048], P('dp')
- output 2: bfloat16 [64, 8, 64], P('dp', 'tp')
- output 3: bfloat16 [64, 8, 64], P('dp', 'tp')
All inputs are finite; a program needn't handle non-finite values.
Results may differ from a plain program's by a relative error of at most 0.0128287.
Values sent between devices are 32-bit elements.
A program may use at most 1 GiB of HBM per device.

v0:
```python
import math
import jax
import jax.numpy as jnp
from jax import lax
from jax.experimental import pallas as pl
from jax.experimental.pallas import tpu as pltpu
from jax.sharding import PartitionSpec as P

NORM_EPS = 1e-5
ROPE_THETA = 500000.0
MASK_VALUE = -1e30
LANES = 128
SLOTS = 4
SCALE = 0.125


def rope_freqs(head_dim):
    freq_list = []
    for index in range(head_dim // 2):
        base_freq = 1.0 / (ROPE_THETA ** (2.0 * index / head_dim))
        wave_len = 2.0 * math.pi / base_freq
        if wave_len < 2048.0:
            freq_list.append(base_freq)
        elif wave_len > 8192.0:
            freq_list.append(base_freq / 8.0)
        else:
            smooth = (8192.0 / wave_len - 1.0) / 3.0
            freq_list.append((1.0 - smooth) * base_freq / 8.0 + smooth * base_freq)
    return jnp.array(freq_list, dtype=jnp.float32)


MESH_ID = pl.DeviceIdType.MESH
CHUNKS = 4
ANY = pl.BlockSpec(memory_space=pl.ANY)
VMEM = pl.BlockSpec(memory_space=pltpu.VMEM)
SMEM = pl.BlockSpec(memory_space=pltpu.SMEM)
GROUP_ROWS = 8
BIG_VMEM = 60 * 1024 * 1024


def neighbours():
    row = lax.axis_index('kv')
    place = lax.axis_index('tp')
    core = lax.rem(place, 2)
    return row, core, {'tp': place + 1 - 2 * core}, {'tp': lax.rem(place + 2, 4)}, {'kv': 1 - row}


def greet(barrier, peers):
    for peer in peers:
        pl.semaphore_signal(barrier, inc=1, device_id=peer, device_id_type=MESH_ID)


def remote(src, dst, sems, index, peer):
    return pltpu.make_async_remote_copy(src_ref=src, dst_ref=dst, send_sem=sems.at[(0,) + index], recv_sem=sems.at[(1,) + index],
                                        device_id=peer, device_id_type=MESH_ID)


def reduce_chips(produce, part, from_core, chip, from_chip, sems, core, other_core, other_chip):
    first, second = [], []
    for j in range(CHUNKS):
        block = produce(j)
        width = block.shape[1] // 2
        part[j, 0] = block[:, :width]
        part[j, 1] = block[:, width:]
        copy = remote(part.at[j, 1 - core], from_core.at[j], sems, (0, j), other_core)
        copy.start()
        first.append(copy)
    for j in range(CHUNKS):
        first[j].wait_recv()
        chip[j] = part[j, core] + from_core[j]
        copy = remote(chip.at[j], from_chip.at[j], sems, (1, j), other_chip)
        copy.start()
        second.append(copy)
    return first, second


def all_reduce(produce, part, from_core, chip, from_chip, total, sems, core, other_core, other_chip):
    first, second = reduce_chips(produce, part, from_core, chip, from_chip, sems, core, other_core, other_chip)
    third = []
    for j in range(CHUNKS):
        second[j].wait_recv()
        total[j, core] = chip[j] + from_chip[j]
        copy = remote(total.at[j, core], total.at[j, core], sems, (2, j), other_core)
        copy.start()
        third.append(copy)
    for copy in third:
        copy.wait_recv()
    return first + second + third


def norm_chunks(chunks, gains_ref, index):
    width = chunks[0].shape[1]
    square = sum(jnp.sum(c * c, axis=1, keepdims=True) for c in chunks)
    inv = lax.rsqrt(square / (width * len(chunks)) + NORM_EPS)
    return jnp.concatenate([(c * inv * gains_ref[index:index + 1, k * width:(k + 1) * width]).astype(jnp.bfloat16)
                            for k, c in enumerate(chunks)], axis=1)


def swiglu_hidden(u_ref, wg_ref, wu_ref, act_ref):
    block = 512
    for n in range(wg_ref.shape[1] // block):
        cols = pl.ds(n * block, block)
        gate = jnp.dot(u_ref[...], wg_ref[:, cols], preferred_element_type=jnp.float32)
        upper = jnp.dot(u_ref[...], wu_ref[:, cols], preferred_element_type=jnp.float32)
        act_ref[:, cols] = (jax.nn.silu(gate) * upper).astype(jnp.bfloat16)


def chunk_dot(lhs_ref, w_ref):
    block = w_ref.shape[1] // CHUNKS
    return lambda j: jnp.dot(lhs_ref[...], w_ref[:, j * block:(j + 1) * block], preferred_element_type=jnp.float32)


def half_lane(shape):
    return lax.broadcasted_iota(jnp.int32, shape, 1) < shape[1] // 2


def half_sums(value):
    low = half_lane(value.shape)
    return jnp.where(low, jnp.sum(jnp.where(low, value, 0.0), axis=1, keepdims=True),
                     jnp.sum(jnp.where(low, 0.0, value), axis=1, keepdims=True))


def by_group(columns, group):
    low = half_lane(columns[0].shape)
    out = []
    for g in range(group):
        a, b = columns[g // 2], columns[group // 2 + g // 2]
        if g % 2 == 0:
            out.append(jnp.where(low, a, pltpu.roll(b, b.shape[1] // 2, 1)))
        else:
            out.append(jnp.where(low, pltpu.roll(a, a.shape[1] // 2, 1), b))
    return out


def store_block_diagonal(ref, groups, lead=()):
    rows, lanes = groups[0].shape
    low = half_lane((rows, lanes))
    for g, value in enumerate(groups):
        ref[lead + (pl.ds(g, rows, stride=8), slice(None))] = jnp.where(low, value, 0.0)
        ref[lead + (pl.ds(4 + g, rows, stride=8), slice(None))] = jnp.where(low, 0.0, value)


def load_groups(ref, lead, rows, lanes, group):
    low = half_lane((rows, lanes))
    return [jnp.where(low, ref[lead, pl.ds(g, rows, stride=8), :], ref[lead, pl.ds(4 + g, rows, stride=8), :]) for g in range(group)]


def pack_partial(tx, outs, tops, totals):
    group = len(outs)
    lane = lax.rem(lax.broadcasted_iota(jnp.int32, outs[0].shape, 1), outs[0].shape[1] // 2)
    packed = jnp.zeros_like(outs[0])
    for g in range(group):
        tx[g] = outs[g]
        packed = jnp.where(lane == g, tops[g], packed)
        packed = jnp.where(lane == group + g, totals[g], packed)
    tx[group] = packed


def unpack_partial(rx, group):
    packed = rx[group]
    low = half_lane(packed.shape)
    middle = packed.shape[1] // 2

    def spread(k):
        return jnp.where(low, jnp.broadcast_to(packed[:, k:k + 1], packed.shape), jnp.broadcast_to(packed[:, middle + k:middle + k + 1], packed.shape))

    return [rx[g] for g in range(group)], [spread(g) for g in range(group)], [spread(group + g) for g in range(group)]


def merge(parts):
    best = parts[0][1]
    for _, top, _ in parts[1:]:
        best = jnp.maximum(best, top)
    out, total = 0.0, 0.0
    for value, top, count in parts:
        weight = jnp.exp(top - best)
        out = out + value * weight
        total = total + count * weight
    return out / jnp.where(total > 0, total, 1.0)


def load_projection(w_hbm, w_ref, sems, group, head_dim):
    out = []
    for g in range(group):
        for h in range(2):
            out.append(pltpu.make_async_copy(w_hbm.at[pl.ds((h * group + g) * head_dim, head_dim), :],
                                             w_ref.at[pl.ds((g * 2 + h) * head_dim, head_dim), :], sems.at[g * 2 + h]))
    return out


def self_layer(x, keys, values, seq_len, gains, wq, wk, wv, wo, wg, wu, wd, wqc, group):
    batch, width = x.shape
    feat = wk.shape[1]
    head_dim = feat // 2
    slots = keys.shape[1]
    mine = batch // 2
    ff = wg.shape[1]
    qcols = wq.shape[1]
    loads = batch // GROUP_ROWS
    chunk = width // CHUNKS // 2

    def kernel(seq_ref, x_ref, gains_ref, k_hbm, v_hbm, wq_hbm, wk_hbm, wv_hbm, wo_hbm, wg_hbm, wu_hbm, wd_hbm, wqc_hbm,
               kn_ref, vn_ref, qx_ref, h_ref,
               wq_ref, wk_ref, wv_ref, kbuf, vbuf, wo_ref, wg_ref, wu_ref, wd_ref, wqc_ref,
               seqf, qg_ref, knf, vnf, q3_ref, o_ref, m_ref, l_ref, tx, rx, att_ref, u_ref, act_ref,
               part, from_core, chip, from_chip, total, qtx, qrx,
               wsem, ksem, vsem, osem, red_sems, pair_sems):
        row, core, other_core, other_chip, other_row = neighbours()
        barrier = pltpu.get_barrier_semaphore()
        greet(barrier, (other_core, other_chip, other_row))

        def fetch(src, dst, index):
            copy = pltpu.make_async_copy(src, dst, wsem.at[index])
            copy.start()
            return copy

        c_q, c_k, c_v = fetch(wq_hbm, wq_ref, 0), fetch(wk_hbm, wk_ref, 1), fetch(wv_hbm, wv_ref, 2)

        def cache_copies(index):
            start = lax.rem((1 - row) * mine + index * GROUP_ROWS, batch)
            rows = pl.ds(pl.multiple_of(start * feat, GROUP_ROWS * feat), GROUP_ROWS * feat)
            return (pltpu.make_async_copy(k_hbm.at[rows, :], kbuf.at[rows, :], ksem.at[index]),
                    pltpu.make_async_copy(v_hbm.at[rows, :], vbuf.at[rows, :], vsem.at[index]))

        for index in range(loads):
            for copy in cache_copies(index):
                copy.start()
        c_o = load_projection(wo_hbm, wo_ref, osem, group, head_dim)
        for copy in c_o:
            copy.start()
        c_g, c_u, c_d = fetch(wg_hbm, wg_ref, 3), fetch(wu_hbm, wu_ref, 4), fetch(wd_hbm, wd_ref, 5)
        c_qc = fetch(wqc_hbm, wqc_ref, 6)

        for b in range(batch):
            seqf[b:b + 1, :] = jnp.full((1, feat), seq_ref[b].astype(jnp.float32))
        angles = seqf[...] * gains_ref[5:6, :feat]
        lane = lax.rem(lax.broadcasted_iota(jnp.int32, (batch, feat), 1), head_dim)
        first = lane < head_dim // 2
        cos_t = jnp.cos(angles)
        sin_t = jnp.where(first, -jnp.sin(angles), jnp.sin(angles))

        def rope(value):
            partner = jnp.where(first, pltpu.roll(value, feat - head_dim // 2, 1), pltpu.roll(value, head_dim // 2, 1))
            return (value * cos_t + partner * sin_t).astype(jnp.bfloat16).astype(jnp.float32)

        x_float = x_ref[...].astype(jnp.float32)
        inv = lax.rsqrt(jnp.mean(x_float * x_float, axis=1, keepdims=True) + NORM_EPS)
        x_norm = (x_float * inv * gains_ref[0:1, :]).astype(jnp.bfloat16)
        c_q.wait()
        query = jnp.dot(x_norm, wq_ref[...], preferred_element_type=jnp.float32)
        groups = by_group([rope(query[:, n * feat:(n + 1) * feat]) for n in range(qcols // feat)], group)
        for g in range(group):
            qg_ref[g] = groups[g]
        store_block_diagonal(q3_ref, groups)
        c_k.wait()
        key_new = rope(jnp.dot(x_norm, wk_ref[...], preferred_element_type=jnp.float32))
        c_v.wait()
        val_new = jnp.dot(x_norm, wv_ref[...], preferred_element_type=jnp.float32).astype(jnp.bfloat16)
        kn_ref[...] = key_new.astype(jnp.bfloat16)
        vn_ref[...] = val_new
        knf[...] = key_new
        vnf[...] = val_new.astype(jnp.float32)

        def attend(phase, start, local):
            q_a = q3_ref[pl.ds(pl.multiple_of(start * 8, 16), 8), :]
            q_b = q3_ref[pl.ds(pl.multiple_of(start * 8, 16) + 8, 8), :]
            zero = jnp.zeros_like(q_a)
            q_pair = jnp.concatenate([jnp.concatenate([q_a, zero], axis=1), jnp.concatenate([zero, q_b], axis=1)], axis=0).astype(jnp.bfloat16)
            rows = pl.ds(pl.multiple_of(start * feat, 2 * feat), 2 * feat)
            scores = jnp.dot(q_pair, kbuf[rows, :], preferred_element_type=jnp.float32)
            slot = lax.broadcasted_iota(jnp.int32, scores.shape, 1)
            sub = lax.broadcasted_iota(jnp.int32, scores.shape, 0)
            visible = slot < jnp.where(sub < 8, seq_ref[start], seq_ref[start + 1]) - row * slots
            scores = jnp.where(visible, scores, MASK_VALUE)
            top = jnp.max(scores, axis=1, keepdims=True)
            probs = jnp.where(visible, jnp.exp((scores - top) * SCALE), 0.0)
            count = jnp.sum(probs, axis=1, keepdims=True)
            out = lax.dot_general(probs.astype(jnp.bfloat16), vbuf[rows, :], (((1,), (1,)), ((), ())), preferred_element_type=jnp.float32)
            for half in range(2):
                where = pl.ds(pl.multiple_of(local * 8, 16) + 8 * half, 8)
                o_ref[phase, where, :] = out[8 * half:8 * half + 8, feat * half:feat * half + feat]
                m_ref[phase, where, :] = jnp.broadcast_to(top[8 * half:8 * half + 8] * SCALE, (8, feat))
                l_ref[phase, where, :] = jnp.broadcast_to(count[8 * half:8 * half + 8], (8, feat))

        def attend_half(phase):
            def body(index, carry):
                k_copy, v_copy = cache_copies(phase * (loads // 2) + index)
                k_copy.wait()
                v_copy.wait()
                start = lax.rem((1 - row) * mine + (phase * (loads // 2) + index) * GROUP_ROWS, batch)
                for p in range(GROUP_ROWS // 2):
                    attend(phase, start + 2 * p, index * GROUP_ROWS + 2 * p)
                return carry

            lax.fori_loop(0, loads // 2, body, 0)

        attend_half(0)
        pack_partial(tx, *(load_groups(ref, 0, mine, feat, group) for ref in (o_ref, m_ref, l_ref)))
        pl.semaphore_wait(barrier, 3)
        sent = remote(tx, rx, pair_sems, (0,), other_row)
        sent.start()
        attend_half(1)

        own = pl.ds(pl.multiple_of(row * mine, mine), mine)
        key_own, val_own = knf[own, :], vnf[own, :]
        outs, tops, counts = (load_groups(ref, 1, mine, feat, group) for ref in (o_ref, m_ref, l_ref))
        new_tops = [half_sums(qg_ref[g, own, :] * key_own) * SCALE for g in range(group)]
        sent.wait_recv()
        outs_p, tops_p, counts_p = unpack_partial(rx, group)
        for g in range(group):
            merged = merge(((outs[g], tops[g], counts[g]), (outs_p[g], tops_p[g], counts_p[g]), (val_own, new_tops[g], 1.0)))
            att_ref[:, g * feat:(g + 1) * feat] = merged.astype(jnp.bfloat16)
        for copy in c_o:
            copy.wait()
        pending = [sent]
        ends = (core, other_core, other_chip)
        pending += all_reduce(chunk_dot(att_ref, wo_ref), part.at[0], from_core.at[0], chip.at[0], from_chip.at[0], total.at[0], red_sems.at[0], *ends)
        cols = [slice(k * chunk, (k + 1) * chunk) for k in range(2 * CHUNKS)]
        hidden = [(x_ref[own, cols[k]].astype(jnp.float32) + total[0, k // 2, k % 2]).astype(jnp.bfloat16).astype(jnp.float32) for k in range(2 * CHUNKS)]
        for k in range(2 * CHUNKS):
            h_ref[k] = hidden[k]
        u_ref[...] = norm_chunks(hidden, gains_ref, 1)
        c_g.wait()
        c_u.wait()
        swiglu_hidden(u_ref, wg_ref, wu_ref, act_ref)
        c_d.wait()
        pending += all_reduce(chunk_dot(act_ref, wd_ref), part.at[1], from_core.at[1], chip.at[1], from_chip.at[1], total.at[1], red_sems.at[1], *ends)
        hidden = [(h_ref[k] + total[1, k // 2, k % 2]).astype(jnp.bfloat16).astype(jnp.float32) for k in range(2 * CHUNKS)]
        for k in range(2 * CHUNKS):
            h_ref[k] = hidden[k]
        u_ref[...] = norm_chunks(hidden, gains_ref, 2)
        c_qc.wait()
        query = jnp.dot(u_ref[...], wqc_ref[...], preferred_element_type=jnp.float32)
        groups = by_group([query[:, n * feat:(n + 1) * feat] for n in range(qcols // feat)], group)
        groups = [(v * lax.rsqrt(half_sums(v * v) / head_dim + NORM_EPS) * gains_ref[4:5, :feat]).astype(jnp.bfloat16).astype(jnp.float32) for v in groups]
        for g in range(group):
            qtx[g] = groups[g]
        sent = remote(qtx, qrx, pair_sems, (1,), other_row)
        sent.start()
        pending.append(sent)
        store_block_diagonal(qx_ref, groups, (row,))
        sent.wait_recv()
        store_block_diagonal(qx_ref, [qrx[g] for g in range(group)], (1 - row,))
        for copy in pending:
            copy.wait_send()

    bf16, f32 = jnp.bfloat16, jnp.float32
    chunk_shape = (2, CHUNKS, mine, chunk)
    return pl.pallas_call(
        kernel,
        out_shape=(jax.ShapeDtypeStruct((batch, feat), bf16), jax.ShapeDtypeStruct((batch, feat), bf16),
                   jax.ShapeDtypeStruct((2, mine * 8, feat), f32), jax.ShapeDtypeStruct((2 * CHUNKS, mine, chunk), f32)),
        in_specs=[SMEM, VMEM, VMEM] + [ANY] * 10,
        out_specs=(VMEM,) * 4,
        scratch_shapes=[pltpu.VMEM(wq.shape, bf16), pltpu.VMEM(wk.shape, bf16), pltpu.VMEM(wv.shape, bf16),
                        pltpu.VMEM(keys.shape, bf16), pltpu.VMEM(values.shape, bf16), pltpu.VMEM(wo.shape, bf16),
                        pltpu.VMEM(wg.shape, bf16), pltpu.VMEM(wu.shape, bf16), pltpu.VMEM(wd.shape, bf16), pltpu.VMEM(wqc.shape, bf16),
                        pltpu.VMEM((batch, feat), f32), pltpu.VMEM((group, batch, feat), f32), pltpu.VMEM((batch, feat), f32), pltpu.VMEM((batch, feat), f32),
                        pltpu.VMEM((batch * 8, feat), f32)] + [pltpu.VMEM((2, mine * 8, feat), f32)] * 3
                       + [pltpu.VMEM((group + 1, mine, feat), f32)] * 2
                       + [pltpu.VMEM((mine, group * feat), bf16), pltpu.VMEM((mine, width), bf16), pltpu.VMEM((mine, ff), bf16)]
                       + [pltpu.VMEM((2, CHUNKS, 2, mine, chunk), f32)] + [pltpu.VMEM(chunk_shape, f32)] * 3 + [pltpu.VMEM((2, CHUNKS, 2, mine, chunk), f32)]
                       + [pltpu.VMEM((group, mine, feat), f32)] * 2
                       + [pltpu.SemaphoreType.DMA((7,)), pltpu.SemaphoreType.DMA((loads,)), pltpu.SemaphoreType.DMA((loads,)), pltpu.SemaphoreType.DMA((2 * group,)),
                          pltpu.SemaphoreType.DMA((2, 2, 3, CHUNKS)), pltpu.SemaphoreType.DMA((2, 2))],
        compiler_params=pltpu.CompilerParams(vmem_limit_bytes=BIG_VMEM, collective_id=1, has_side_effects=True),
        cost_estimate=pl.CostEstimate(flops=2 * batch * width * (3 * ff + 3 * qcols), bytes_accessed=50 * 1024 * 1024, transcendentals=batch * 8 * slots),
        name='self_layer',
    )(seq_len, x, gains, keys, values, wq, wk, wv, wo, wg, wu, wd, wqc)


def cross_tail(outs_in, tops_in, totals_in, hidden_in, tile_rows, gates, gains, wo, wg, wu, wd, group):
    mine = hidden_in.shape[1]
    feat = outs_in.shape[2]
    head_dim = feat // 2
    width, ff = wg.shape
    tiles = tile_rows.shape[0]
    chunk = width // CHUNKS // 2

    def kernel(tile_ref, gate_ref, o_ref, m_ref, l_ref, h_ref, gains_ref, wo_hbm, wg_hbm, wu_hbm, wd_hbm, out_ref,
               wo_ref, wg_ref, wu_ref, wd_ref, on_ref, h3_ref, tx, rx, att_ref, u_ref, act_ref,
               part, from_core, chip, from_chip, total, final,
               wsem, osem, red_sems, pair_sems, far_sems):
        row, core, other_core, other_chip, other_row = neighbours()
        barrier = pltpu.get_barrier_semaphore()
        greet(barrier, (other_core, other_chip, other_row))
        c_o = load_projection(wo_hbm, wo_ref, osem, group, head_dim)
        for copy in c_o:
            copy.start()
        c_w = [pltpu.make_async_copy(src, dst, wsem.at[i]) for i, (src, dst) in enumerate(((wg_hbm, wg_ref), (wu_hbm, wu_ref), (wd_hbm, wd_ref)))]
        for copy in c_w:
            copy.start()
        pack_partial(tx, *(load_groups(ref, 1 - row, mine, feat, group) for ref in (o_ref, m_ref, l_ref)))
        pl.semaphore_wait(barrier, 3)
        sent = remote(tx, rx, pair_sems, (0,), other_row)
        sent.start()
        for r in range(mine):
            seen = tile_ref[0, row * mine + r]
            for t in range(1, tiles):
                seen = jnp.maximum(seen, tile_ref[t, row * mine + r])
            on_ref[r:r + 1, :] = jnp.full((1, chunk), jnp.where(seen != 0, 1.0, 0.0))
        gate_att = jnp.tanh(jnp.full((1, chunk), gate_ref[0]))
        gate_mlp = jnp.tanh(jnp.full((1, chunk), gate_ref[1]))
        outs, tops, counts = (load_groups(ref, row, mine, feat, group) for ref in (o_ref, m_ref, l_ref))
        sent.wait_recv()
        outs_p, tops_p, counts_p = unpack_partial(rx, group)
        for g in range(group):
            merged = merge(((outs[g], tops[g], counts[g]), (outs_p[g], tops_p[g], counts_p[g])))
            att_ref[:, g * feat:(g + 1) * feat] = merged.astype(jnp.bfloat16)
        for copy in c_o:
            copy.wait()
        pending = [sent]
        ends = (core, other_core, other_chip)
        pending += all_reduce(chunk_dot(att_ref, wo_ref), part.at[0], from_core.at[0], chip.at[0], from_chip.at[0], total, red_sems.at[0], *ends)
        hidden = [(h_ref[k] + gate_att * on_ref[...] * total[k // 2, k % 2]).astype(jnp.bfloat16).astype(jnp.float32) for k in range(2 * CHUNKS)]
        for k in range(2 * CHUNKS):
            h3_ref[k] = hidden[k]
        u_ref[...] = norm_chunks(hidden, gains_ref, 3)
        c_w[0].wait()
        c_w[1].wait()
        swiglu_hidden(u_ref, wg_ref, wu_ref, act_ref)
        c_w[2].wait()
        first, second = reduce_chips(chunk_dot(act_ref, wd_ref), part.at[1], from_core.at[1], chip.at[1], from_chip.at[1], red_sems.at[1], *ends)
        pending += first + second
        near, far, relay = [], [], []
        for j in range(CHUNKS):
            second[j].wait_recv()
            summed = chip[1, j] + from_chip[1, j]
            final[row, 2 * j + core] = (h3_ref[2 * j + core] + gate_mlp * on_ref[...] * summed).astype(jnp.bfloat16).astype(jnp.float32)
            piece = final.at[row, 2 * j + core]
            far.append(remote(piece, piece, far_sems, (0, j), other_row))
            far[j].start()
            near.append(remote(piece, piece, far_sems, (1, j), other_core))
            near[j].start()
        for j in range(CHUNKS):
            far[j].wait_recv()
            piece = final.at[1 - row, 2 * j + core]
            relay.append(remote(piece, piece, far_sems, (2, j), other_core))
            relay[j].start()
        for j in range(CHUNKS):
            near[j].wait_recv()
        for j in range(CHUNKS):
            relay[j].wait_recv()
        for half in range(2):
            for k in range(2 * CHUNKS):
                out_ref[half * mine:(half + 1) * mine, k * chunk:(k + 1) * chunk] = final[half, k].astype(jnp.bfloat16)
        for copy in pending + near + far + relay:
            copy.wait_send()

    bf16, f32 = jnp.bfloat16, jnp.float32
    chunk_shape = (2, CHUNKS, mine, chunk)
    return pl.pallas_call(
        kernel,
        out_shape=jax.ShapeDtypeStruct((2 * mine, width), bf16),
        in_specs=[SMEM, SMEM] + [VMEM] * 5 + [ANY] * 4,
        out_specs=VMEM,
        scratch_shapes=[pltpu.VMEM(wo.shape, bf16), pltpu.VMEM(wg.shape, bf16), pltpu.VMEM(wu.shape, bf16), pltpu.VMEM(wd.shape, bf16),
                        pltpu.VMEM((mine, chunk), f32), pltpu.VMEM((2 * CHUNKS, mine, chunk), f32)]
                       + [pltpu.VMEM((group + 1, mine, feat), f32)] * 2
                       + [pltpu.VMEM((mine, group * feat), bf16), pltpu.VMEM((mine, width), bf16), pltpu.VMEM((mine, ff), bf16)]
                       + [pltpu.VMEM((2, CHUNKS, 2, mine, chunk), f32)] + [pltpu.VMEM(chunk_shape, f32)] * 3 + [pltpu.VMEM((CHUNKS, 2, mine, chunk), f32)]
                       + [pltpu.VMEM((2, 2 * CHUNKS, mine, chunk), f32)]
                       + [pltpu.SemaphoreType.DMA((3,)), pltpu.SemaphoreType.DMA((2 * group,)),
                          pltpu.SemaphoreType.DMA((2, 2, 3, CHUNKS)), pltpu.SemaphoreType.DMA((2, 1)), pltpu.SemaphoreType.DMA((2, 3, CHUNKS))],
        compiler_params=pltpu.CompilerParams(vmem_limit_bytes=BIG_VMEM, collective_id=2, has_side_effects=True),
        cost_estimate=pl.CostEstimate(flops=4 * mine * width * 3 * ff, bytes_accessed=30 * 1024 * 1024, transcendentals=mine * ff),
        name='cross_tail',
    )(tile_rows, gates, outs_in, tops_in, totals_in, hidden_in, gains, wo, wg, wu, wd)


def cross_attention(query_bd, keys, values, tile_rows):
    rows, feat, tokens = keys.shape
    tiles = tile_rows.shape[0]
    half_tokens = tokens
    tile_tok = half_tokens // 2
    base_one = tile_tok // LANES * LANES
    width = tokens - base_one
    width_pad = width
    width_zero = min(width_pad, -(-tile_tok // LANES) * LANES)

    def kernel(tile_ref, q_ref, k_hbm, v_hbm, o_ref, m_ref, l_ref, list_ref, kbuf, vbuf, ksem, vsem):
        kv_index = lax.axis_index('kv')
        first_tile = kv_index * (tiles // 2)

        def add_zero(row, count):
            list_ref[count] = row
            return count + jnp.where(tile_ref[first_tile, row] != 0, 1, 0)

        def add_one(row, count):
            list_ref[count] = row
            return count + jnp.where(tile_ref[first_tile + 1, row] != 0, 1, 0)

        n_zero = lax.fori_loop(0, rows, add_zero, jnp.int32(0))
        list_ref[n_zero] = list_ref[jnp.maximum(n_zero - 1, 0)]
        pairs_zero = (n_zero + 1) // 2
        start_one = 2 * pairs_zero
        end_one = lax.fori_loop(0, rows, add_one, start_one)
        n_one = end_one - start_one
        list_ref[end_one] = list_ref[jnp.maximum(end_one - 1, 0)]
        pairs = pairs_zero + (n_one + 1) // 2

        def copies(index, is_one):
            slot = lax.rem(index, SLOTS)
            out = []
            for half in range(2):
                row = list_ref[2 * index + half]
                span = pl.ds(base_one, width) if is_one else pl.ds(0, width_zero)
                dest = pl.ds(0, width) if is_one else pl.ds(0, width_zero)
                for hbm, buf, sem in ((k_hbm, kbuf, ksem), (v_hbm, vbuf, vsem)):
                    out.append(pltpu.make_async_copy(
                        hbm.at[row, :, span], buf.at[slot, pl.ds(half * feat, feat), dest], sem.at[slot, half]))
            return out

        def start(index):
            @pl.when(index < pairs_zero)
            def _():
                for copy in copies(index, False):
                    copy.start()

            @pl.when((index >= pairs_zero) & (index < pairs))
            def _():
                for copy in copies(index, True):
                    copy.start()

        def wait(index):
            @pl.when(index < pairs_zero)
            def _():
                for copy in copies(index, False):
                    copy.wait()

            @pl.when(index >= pairs_zero)
            def _():
                for copy in copies(index, True):
                    copy.wait()

        for index in range(SLOTS - 1):
            start(jnp.int32(index))
        o_ref[...] = jnp.zeros_like(o_ref)
        l_ref[...] = jnp.zeros_like(l_ref)
        m_ref[...] = jnp.full_like(m_ref, MASK_VALUE)

        def step(index, carry):
            start(index + SLOTS - 1)
            wait(index)
            slot = lax.rem(index, SLOTS)
            row_a = list_ref[2 * index]
            row_b = list_ref[2 * index + 1]
            is_one = index >= pairs_zero
            low = jnp.where(is_one, tile_tok - base_one, 0)
            high = jnp.where(is_one, width, tile_tok)
            high_b = jnp.where(is_one, jnp.where(2 * index + 1 == end_one, 0, high), jnp.where(2 * index + 1 == n_zero, 0, high))
            q_a = q_ref[pl.ds(pl.multiple_of(row_a * 8, 8), 8), :]
            q_b = q_ref[pl.ds(pl.multiple_of(row_b * 8, 8), 8), :]
            zero = jnp.zeros_like(q_a)
            q_pair = jnp.concatenate([jnp.concatenate([q_a, zero], axis=1), jnp.concatenate([zero, q_b], axis=1)], axis=0).astype(jnp.bfloat16)
            scores = jnp.dot(q_pair, kbuf[slot], preferred_element_type=jnp.float32)
            lane = lax.broadcasted_iota(jnp.int32, scores.shape, 1)
            sub = lax.broadcasted_iota(jnp.int32, scores.shape, 0)
            visible = (lane >= low) & (lane < jnp.where(sub < 8, high, high_b))
            scores = jnp.where(visible, scores, MASK_VALUE)
            top = jnp.max(scores, axis=1, keepdims=True)
            probs = jnp.where(visible, jnp.exp((scores - top) * SCALE), 0.0)
            total = jnp.sum(probs, axis=1, keepdims=True)
            lane_v = lax.broadcasted_iota(jnp.int32, (2 * feat, width - width_zero), 1)
            tail = jnp.where(lane_v < jnp.where(is_one, width, 0), vbuf[slot, :, width_zero:], jnp.zeros((), jnp.bfloat16))
            vals = jnp.concatenate([vbuf[slot, :, :width_zero], tail], axis=1)
            out = lax.dot_general(probs.astype(jnp.bfloat16), vals, (((1,), (1,)), ((), ())), preferred_element_type=jnp.float32)
            for half, row in ((0, row_a), (1, row_b)):
                where = pl.ds(pl.multiple_of(row * 8, 8), 8)
                part = out[8 * half:8 * half + 8, feat * half:feat * half + feat]
                top_new = jnp.broadcast_to(top[8 * half:8 * half + 8] * SCALE, (8, feat))
                total_new = jnp.broadcast_to(total[8 * half:8 * half + 8], (8, feat))
                top_old = m_ref[where, :]
                best = jnp.maximum(top_old, top_new)
                w_old = jnp.exp(top_old - best)
                w_new = jnp.exp(top_new - best)
                m_ref[where, :] = best
                l_ref[where, :] = l_ref[where, :] * w_old + total_new * w_new
                o_ref[where, :] = o_ref[where, :] * w_old + part * w_new
            return carry

        lax.fori_loop(0, pairs, step, 0)

    flat = jax.ShapeDtypeStruct((rows * 8, feat), jnp.float32)
    return pl.pallas_call(
        kernel,
        out_shape=(flat, flat, flat),
        in_specs=[pl.BlockSpec(memory_space=pltpu.SMEM), pl.BlockSpec(memory_space=pltpu.VMEM),
                  pl.BlockSpec(memory_space=pl.ANY), pl.BlockSpec(memory_space=pl.ANY)],
        out_specs=(pl.BlockSpec(memory_space=pltpu.VMEM),) * 3,
        scratch_shapes=[pltpu.SMEM((2 * rows + 8,), jnp.int32),
                        pltpu.VMEM((SLOTS, 2 * feat, width_pad), jnp.bfloat16),
                        pltpu.VMEM((SLOTS, 2 * feat, width_pad), jnp.bfloat16),
                        pltpu.SemaphoreType.DMA((SLOTS, 2)), pltpu.SemaphoreType.DMA((SLOTS, 2))],
        compiler_params=pltpu.CompilerParams(vmem_limit_bytes=40 * 1024 * 1024),
        cost_estimate=pl.CostEstimate(flops=4 * 8 * feat * tokens * rows, bytes_accessed=2 * feat * tokens * rows, transcendentals=8 * tokens * rows),
        name='cross_attention',
    )(tile_rows, query_bd, keys, values)


def solution(mesh):
    rows_spec = P('dp', None)
    cache_spec = P('dp', 'tp', 'kv', None)
    new_spec = P('dp', 'tp', None)
    col_spec = P(None, 'tp')
    row_spec = P('tp', None)
    vec_spec = P(None)
    in_specs = (rows_spec, cache_spec, cache_spec, P('dp'), cache_spec, cache_spec, rows_spec,
                vec_spec, col_spec, col_spec, col_spec, row_spec, vec_spec, col_spec, col_spec, row_spec,
                vec_spec, col_spec, vec_spec, row_spec, vec_spec, vec_spec, col_spec, col_spec, row_spec)
    out_specs = (rows_spec, new_spec, new_spec)

    def device_step(x, ks_cache, vs_cache, seq_len, kx_cache, vx_cache, tile_vis, attn_norm, wq_self, wk_self, wv_self, wo_self, mlp_norm, wg_self, wu_self, wd_self, xattn_norm, wq_cross, q_norm, wo_cross, cross_gates, xmlp_norm, wg_cross, wu_cross, wd_cross):
        batch, width = x.shape
        kv_local, slots, head_dim = ks_cache.shape[1:]
        feat = kv_local * head_dim
        group = wq_self.shape[1] // feat
        tokens = kx_cache.shape[2]
        rows = [attn_norm, mlp_norm, xattn_norm, xmlp_norm, jnp.tile(q_norm, width // head_dim)]
        gains = jnp.stack([r.astype(jnp.float32) for r in rows] + [jnp.tile(rope_freqs(head_dim), 2 * width // head_dim)] + [jnp.zeros((width,), jnp.float32)] * 2)

        def token_minor(cache):
            return jnp.swapaxes(cache, 2, 3).reshape(batch, feat, cache.shape[2])

        key_new, val_new, query_x, h_two = self_layer(
            x, token_minor(ks_cache).reshape(batch * feat, slots), token_minor(vs_cache).reshape(batch * feat, slots), seq_len, gains,
            wq_self, wk_self, wv_self, wo_self, wg_self, wu_self, wd_self, wq_cross, group)
        tile_rows = tile_vis.T
        parts = cross_attention(query_x.reshape(batch * 8, feat), token_minor(kx_cache), token_minor(vx_cache), tile_rows)
        parts = [p.reshape(2, batch * 4, feat) for p in parts]
        h_four = cross_tail(*parts, h_two, tile_rows, cross_gates, gains, wo_cross, wg_cross, wu_cross, wd_cross, group)
        return h_four, key_new.reshape(batch, kv_local, head_dim), val_new.reshape(batch, kv_local, head_dim)

    return jax.shard_map(device_step, mesh=mesh, in_specs=in_specs, out_specs=out_specs, check_vma=False)
```

profile of v0, /device:TPU:0, one launch (start us, length us, event | category | flops | bytes accessed | tf_op | source)
XLA Modules:
  0.0 112.7 jit_solution(17663537669720720558)
XLA Ops:
  0.6 0.7 tile.5
  1.3 0.1 stack_tile.3
  1.4 0.7 tile.4
  2.0 0.1 convert_element_type.19
  2.1 0.7 stack.41
  2.8 0.7 stack.42
  3.5 0.7 stack.43
  4.2 0.7 stack.44
  4.9 0.7 stack.40.gains_ref
  5.6 0.0 copy-start.4
  5.6 42.8 %self_layer.1 = (bf16[64,128]{1,0:T(8,128)(2,1)}, bf16[64,128]{1,0:T(8,128)(2,1)}, f32[2,256,128]{2,1,0:T(8,128)}, f32[8,32,256]{2,1,0:T(8,128)}) custom-call(s32[64]{0:T(128)} %seq_ref.1, bf16[64,2048]{1,0:T(8,128)(2,1)} %x_ref.1, f32[8,2048]{1,0:T(8,128)} %stack.40.gains_ref, bf16[8192,512]{1,0:T(8,128)(2,1)} %bitcast.29, bf16[8192,512]{1,0:T(8,128)(2,1)} %bitcast.30, ...), custom_call_target="tpu_custom_call" | custom-call | flops 2013265920 | bytes 52428800 | tf_op jit(solution)/shard_map/self_layer/pallas_call | solution.py:349
  48.4 0.0 copy-done.4
  48.5 0.0 copy-start
  48.5 0.9 copy-done
  49.4 27.6 %cross_attention.1 = (f32[512,128]{1,0:T(8,128)S(1)}, f32[512,128]{1,0:T(8,128)S(1)}, f32[512,128]{1,0:T(8,128)S(1)}) custom-call(s32[4,64]{1,0:T(4,128)S(1)} %bitcast.26, f32[512,128]{1,0:T(8,128)S(1)} %bitcast.21, bf16[64,128,3202]{2,1,0:T(8,128)(2,1)} %bitcast.27, bf16[64,128,3202]{2,1,0:T(8,128)(2,1)} %bitcast.28), custom_call_target="tpu_custom_call" | custom-call | flops 839385088 | bytes 52461568 | tf_op jit(solution)/shard_map/cross_attention/pallas_call | solution.py:585
  77.0 0.0 copy-start.1
  77.0 0.7 copy-done.1
  77.7 0.0 copy-start.2
  77.7 0.7 copy-done.2
  78.4 0.0 copy-start.3
  78.4 0.7 copy-done.3
  79.1 0.0 copy-start.6
  79.2 0.0 copy-start.5
  79.2 30.5 %cross_tail.1 = bf16[64,2048]{1,0:T(8,128)(2,1)} custom-call(s32[4,64]{1,0:T(4,128)} %bitcast.25, f32[2]{0:T(128)} %gate_ref.1, f32[2,256,128]{2,1,0:T(8,128)} %bitcast.22, f32[2,256,128]{2,1,0:T(8,128)} %bitcast.23, f32[2,256,128]{2,1,0:T(8,128)} %bitcast.24, f32[8,32,256]{2,1,0:T(8,128)} %get-tuple-element.14.h_ref, f32[8,2048]{1,0:T(8,128)} %stack.40.gains_ref, ...), custom_call_target="tpu_custom_call" | custom-call | flops 1610612736 | bytes 31457280 | tf_op jit(solution)/shard_map/cross_tail/pallas_call | solution.py:452
  109.7 0.0 copy-done.6
  109.7 0.7 reshape.49
  110.4 0.0 copy-done.5
  110.4 0.7 reshape.50
  111.1 1.7 %copy.30 = bf16[64,2048]{1,0:T(8,128)(2,1)} copy(bf16[64,2048]{1,0:T(8,128)(2,1)} %cross_tail.1) | data formatting | bytes 524288
  (1 shorter events, 0.0 us)
Async XLA Ops:
  5.6 42.9 %copy-start.4 = (s32[64,4]{0,1:T(4,128)S(1)}, s32[64,4]{0,1:T(4,128)}, u32[]{:S(2)}) copy-start(s32[64,4]{0,1:T(4,128)} %param.32) | copy-start | bytes 3076
  48.5 1.0 copy-start
  77.0 0.7 copy-start.1
  77.7 0.7 copy-start.2
  78.4 0.7 copy-start.3
  79.1 30.5 %copy-start.6 = (bf16[64,128]{1,0:T(8,128)(2,1)S(1)}, bf16[64,128]{1,0:T(8,128)(2,1)}, u32[]{:S(2)}) copy-start(bf16[64,128]{1,0:T(8,128)(2,1)} %get-tuple-element.15) | copy-start | bytes 49156
  79.2 31.2 %copy-start.5 = (bf16[64,128]{1,0:T(8,128)(2,1)S(1)}, bf16[64,128]{1,0:T(8,128)(2,1)}, u32[]{:S(2)}) copy-start(bf16[64,128]{1,0:T(8,128)(2,1)} %get-tuple-element.16) | copy-start | bytes 49156
where the time goes:
time: 114 us; the launch traced here: 113 us
  Pallas kernels  101 us (89%)
  local copies, waits for them, and re-layouts  8.33 us (7%)
  other arithmetic  2.75 us (2%)
    pallas_call x1, Pallas kernels, self_layer(): pl.pallas_call(kernel, out_shape=(jax.ShapeDtypeStruct((batch, feat), bf1...  42.8 us
    pallas_call x1, Pallas kernels, cross_tail(): pl.pallas_call(kernel, out_shape=jax.ShapeDtypeStruct((2 * mine, width),...  30.5 us
    pallas_call x1, Pallas kernels, cross_attention(): pl.pallas_call(kernel, out_shape=(flat, flat, flat), in_specs=[pl.BlockSp...  27.6 us
    unnamed x15, local copies, waits for them, and re-layouts  4.73 us
    another operation x4, other arithmetic, device_step(): jnp.stack([r.astype(jnp.float32) for r in rows] + [jnp.tile(rope_freqs(he...  2.75 us

commit v1 on v0

--- a/solution.py
+++ b/solution.py
@@ -1,3 +1,4 @@
+import functools
 import math
 import jax
 import jax.numpy as jnp
@@ -10,7 +11,7 @@
 ROPE_THETA = 500000.0
 MASK_VALUE = -1e30
 LANES = 128
-SLOTS = 4
+SLOTS = 5
 SCALE = 0.125
 
 
@@ -35,7 +36,10 @@
 VMEM = pl.BlockSpec(memory_space=pltpu.VMEM)
 SMEM = pl.BlockSpec(memory_space=pltpu.SMEM)
 GROUP_ROWS = 8
-BIG_VMEM = 60 * 1024 * 1024
+
+
+def in_hbm(*arrays):
+    return [pltpu.with_memory_space_constraint(a, pltpu.HBM) for a in arrays]
 
 
 def neighbours():
@@ -88,11 +92,17 @@
     return first + second + third
 
 
-def norm_chunks(chunks, gains_ref, index):
+def lane_row(gain_ref):
+    gain = gain_ref[...].astype(jnp.float32)
+    return jnp.concatenate([gain[k:k + 1] for k in range(gain.shape[0])], axis=1)
+
+
+def norm_chunks(chunks, gain_ref):
     width = chunks[0].shape[1]
+    gain = lane_row(gain_ref)
     square = sum(jnp.sum(c * c, axis=1, keepdims=True) for c in chunks)
     inv = lax.rsqrt(square / (width * len(chunks)) + NORM_EPS)
-    return jnp.concatenate([(c * inv * gains_ref[index:index + 1, k * width:(k + 1) * width]).astype(jnp.bfloat16)
+    return jnp.concatenate([(c * inv * gain[:, k * width:(k + 1) * width]).astype(jnp.bfloat16)
                             for k, c in enumerate(chunks)], axis=1)
 
 
@@ -188,7 +198,7 @@
     return out
 
 
-def self_layer(x, keys, values, seq_len, gains, wq, wk, wv, wo, wg, wu, wd, wqc, group):
+def self_layer(x, keys, values, seq_len, gains, freqs, wq, wk, wv, wo, wg, wu, wd, wqc, group):
     batch, width = x.shape
     feat = wk.shape[1]
     head_dim = feat // 2
@@ -199,15 +209,20 @@
     loads = batch // GROUP_ROWS
     chunk = width // CHUNKS // 2
 
-    def kernel(seq_ref, x_ref, gains_ref, k_hbm, v_hbm, wq_hbm, wk_hbm, wv_hbm, wo_hbm, wg_hbm, wu_hbm, wd_hbm, wqc_hbm,
+    def kernel(seq_ref, x_hbm, ga_hbm, gm_hbm, gx_hbm, gq_hbm, f_hbm, k_hbm, v_hbm, wq_hbm, wk_hbm, wv_hbm, wo_hbm, wg_hbm, wu_hbm, wd_hbm, wqc_hbm,
                kn_ref, vn_ref, qx_ref, h_ref,
-               wq_ref, wk_ref, wv_ref, kbuf, vbuf, wo_ref, wg_ref, wu_ref, wd_ref, wqc_ref,
-               seqf, qg_ref, knf, vnf, q3_ref, o_ref, m_ref, l_ref, tx, rx, att_ref, u_ref, act_ref,
+               x_ref, ga_ref, gm_ref, gx_ref, gq_ref, f_ref, wq_ref, wk_ref, wv_ref, kbuf, vbuf, wo_ref, wg_ref, wu_ref, wd_ref, wqc_ref,
+               seqf, qg_ref, q3_ref, o_ref, m_ref, l_ref, tx, rx, att_ref, u_ref, act_ref,
                part, from_core, chip, from_chip, total, qtx, qrx,
-               wsem, ksem, vsem, osem, red_sems, pair_sems):
+               xsem, wsem, ksem, vsem, osem, red_sems, pair_sems):
         row, core, other_core, other_chip, other_row = neighbours()
         barrier = pltpu.get_barrier_semaphore()
         greet(barrier, (other_core, other_chip, other_row))
+
+        small = [pltpu.make_async_copy(src, dst, xsem.at[i]) for i, (src, dst) in enumerate(
+            ((f_hbm, f_ref), (ga_hbm, ga_ref), (x_hbm, x_ref), (gm_hbm, gm_ref), (gx_hbm, gx_ref), (gq_hbm, gq_ref)))]
+        for copy in small:
+            copy.start()
 
         def fetch(src, dst, index):
             copy = pltpu.make_async_copy(src, dst, wsem.at[index])
@@ -222,18 +237,20 @@
             return (pltpu.make_async_copy(k_hbm.at[rows, :], kbuf.at[rows, :], ksem.at[index]),
                     pltpu.make_async_copy(v_hbm.at[rows, :], vbuf.at[rows, :], vsem.at[index]))
 
-        for index in range(loads):
-            for copy in cache_copies(index):
-                copy.start()
+        def start_cache(quarter):
+            for index in range(quarter * loads // 4, (quarter + 1) * loads // 4):
+                for copy in cache_copies(index):
+                    copy.start()
+
         c_o = load_projection(wo_hbm, wo_ref, osem, group, head_dim)
-        for copy in c_o:
-            copy.start()
-        c_g, c_u, c_d = fetch(wg_hbm, wg_ref, 3), fetch(wu_hbm, wu_ref, 4), fetch(wd_hbm, wd_ref, 5)
-        c_qc = fetch(wqc_hbm, wqc_ref, 6)
-
+        c_g, c_u, c_d, c_qc = (pltpu.make_async_copy(src, dst, wsem.at[3 + i]) for i, (src, dst) in enumerate(
+            ((wg_hbm, wg_ref), (wu_hbm, wu_ref), (wd_hbm, wd_ref), (wqc_hbm, wqc_ref))))
+        start_cache(0)
         for b in range(batch):
             seqf[b:b + 1, :] = jnp.full((1, feat), seq_ref[b].astype(jnp.float32))
-        angles = seqf[...] * gains_ref[5:6, :feat]
+        for copy in small:
+            copy.wait()
+        angles = seqf[...] * f_ref[...]
         lane = lax.rem(lax.broadcasted_iota(jnp.int32, (batch, feat), 1), head_dim)
         first = lane < head_dim // 2
         cos_t = jnp.cos(angles)
@@ -245,8 +262,9 @@
 
         x_float = x_ref[...].astype(jnp.float32)
         inv = lax.rsqrt(jnp.mean(x_float * x_float, axis=1, keepdims=True) + NORM_EPS)
-        x_norm = (x_float * inv * gains_ref[0:1, :]).astype(jnp.bfloat16)
+        x_norm = (x_float * inv * lane_row(ga_ref)).astype(jnp.bfloat16)
         c_q.wait()
+        start_cache(1)
         query = jnp.dot(x_norm, wq_ref[...], preferred_element_type=jnp.float32)
         groups = by_group([rope(query[:, n * feat:(n + 1) * feat]) for n in range(qcols // feat)], group)
         for g in range(group):
@@ -256,10 +274,8 @@
         key_new = rope(jnp.dot(x_norm, wk_ref[...], preferred_element_type=jnp.float32))
         c_v.wait()
         val_new = jnp.dot(x_norm, wv_ref[...], preferred_element_type=jnp.float32).astype(jnp.bfloat16)
-        kn_ref[...] = key_new.astype(jnp.bfloat16)
-        vn_ref[...] = val_new
-        knf[...] = key_new
-        vnf[...] = val_new.astype(jnp.float32)
+        kn_ref[...] = key_new
+        vn_ref[...] = val_new.astype(jnp.float32)
 
         def attend(phase, start, local):
             q_a = q3_ref[pl.ds(pl.multiple_of(start * 8, 16), 8), :]
@@ -277,32 +293,38 @@
             count = jnp.sum(probs, axis=1, keepdims=True)
             out = lax.dot_general(probs.astype(jnp.bfloat16), vbuf[rows, :], (((1,), (1,)), ((), ())), preferred_element_type=jnp.float32)
             for half in range(2):
-                where = pl.ds(pl.multiple_of(local * 8, 16) + 8 * half, 8)
+                where = pl.ds(local * 8 + 8 * half, 8)
                 o_ref[phase, where, :] = out[8 * half:8 * half + 8, feat * half:feat * half + feat]
                 m_ref[phase, where, :] = jnp.broadcast_to(top[8 * half:8 * half + 8] * SCALE, (8, feat))
                 l_ref[phase, where, :] = jnp.broadcast_to(count[8 * half:8 * half + 8], (8, feat))
 
-        def attend_half(phase):
-            def body(index, carry):
-                k_copy, v_copy = cache_copies(phase * (loads // 2) + index)
-                k_copy.wait()
-                v_copy.wait()
-                start = lax.rem((1 - row) * mine + (phase * (loads // 2) + index) * GROUP_ROWS, batch)
-                for p in range(GROUP_ROWS // 2):
-                    attend(phase, start + 2 * p, index * GROUP_ROWS + 2 * p)
-                return carry
-
-            lax.fori_loop(0, loads // 2, body, 0)
-
-        attend_half(0)
+        def attend_quarter(quarter, following):
+            for index in range(quarter * loads // 4, (quarter + 1) * loads // 4):
+                for copy in cache_copies(index):
+                    copy.wait()
+            following()
+            phase, part_rows = quarter // 2, mine // 2
+            start = lax.rem((1 + phase - row) * mine, batch)
+            for p in range(part_rows // 2):
+                local = (quarter % 2) * part_rows + 2 * p
+                attend(phase, start + local, local)
+
+        def start_all(*copies):
+            for copy in copies:
+                copy.start()
+
+        attend_quarter(0, lambda: start_cache(2))
+        attend_quarter(1, lambda: start_cache(3))
         pack_partial(tx, *(load_groups(ref, 0, mine, feat, group) for ref in (o_ref, m_ref, l_ref)))
         pl.semaphore_wait(barrier, 3)
         sent = remote(tx, rx, pair_sems, (0,), other_row)
         sent.start()
-        attend_half(1)
+        attend_quarter(2, lambda: start_all(*c_o, c_g))
+        attend_quarter(3, lambda: start_all(c_u))
+        start_all(c_d, c_qc)
 
         own = pl.ds(pl.multiple_of(row * mine, mine), mine)
-        key_own, val_own = knf[own, :], vnf[own, :]
+        key_own, val_own = kn_ref[own, :], vn_ref[own, :]
         outs, tops, counts = (load_groups(ref, 1, mine, feat, group) for ref in (o_ref, m_ref, l_ref))
         new_tops = [half_sums(qg_ref[g, own, :] * key_own) * SCALE for g in range(group)]
         sent.wait_recv()
@@ -319,7 +341,7 @@
         hidden = [(x_ref[own, cols[k]].astype(jnp.float32) + total[0, k // 2, k % 2]).astype(jnp.bfloat16).astype(jnp.float32) for k in range(2 * CHUNKS)]
         for k in range(2 * CHUNKS):
             h_ref[k] = hidden[k]
-        u_ref[...] = norm_chunks(hidden, gains_ref, 1)
+        u_ref[...] = norm_chunks(hidden, gm_ref)
         c_g.wait()
         c_u.wait()
         swiglu_hidden(u_ref, wg_ref, wu_ref, act_ref)
@@ -328,11 +350,12 @@
         hidden = [(h_ref[k] + total[1, k // 2, k % 2]).astype(jnp.bfloat16).astype(jnp.float32) for k in range(2 * CHUNKS)]
         for k in range(2 * CHUNKS):
             h_ref[k] = hidden[k]
-        u_ref[...] = norm_chunks(hidden, gains_ref, 2)
+        u_ref[...] = norm_chunks(hidden, gx_ref)
         c_qc.wait()
         query = jnp.dot(u_ref[...], wqc_ref[...], preferred_element_type=jnp.float32)
         groups = by_group([query[:, n * feat:(n + 1) * feat] for n in range(qcols // feat)], group)
-        groups = [(v * lax.rsqrt(half_sums(v * v) / head_dim + NORM_EPS) * gains_ref[4:5, :feat]).astype(jnp.bfloat16).astype(jnp.float32) for v in groups]
+        gain = jnp.concatenate([gq_ref[...].astype(jnp.float32)] * 2, axis=1)
+        groups = [(v * lax.rsqrt(half_sums(v * v) / head_dim + NORM_EPS) * gain).astype(jnp.bfloat16).astype(jnp.float32) for v in groups]
         for g in range(group):
             qtx[g] = groups[g]
         sent = remote(qtx, qrx, pair_sems, (1,), other_row)
@@ -348,51 +371,52 @@
     chunk_shape = (2, CHUNKS, mine, chunk)
     return pl.pallas_call(
         kernel,
-        out_shape=(jax.ShapeDtypeStruct((batch, feat), bf16), jax.ShapeDtypeStruct((batch, feat), bf16),
+        out_shape=(jax.ShapeDtypeStruct((batch, feat), f32), jax.ShapeDtypeStruct((batch, feat), f32),
                    jax.ShapeDtypeStruct((2, mine * 8, feat), f32), jax.ShapeDtypeStruct((2 * CHUNKS, mine, chunk), f32)),
-        in_specs=[SMEM, VMEM, VMEM] + [ANY] * 10,
+        in_specs=[SMEM] + [ANY] * 16,
         out_specs=(VMEM,) * 4,
-        scratch_shapes=[pltpu.VMEM(wq.shape, bf16), pltpu.VMEM(wk.shape, bf16), pltpu.VMEM(wv.shape, bf16),
+        scratch_shapes=[pltpu.VMEM(a.shape, a.dtype) for a in (x, *gains, freqs)]
+                       + [pltpu.VMEM(wq.shape, bf16), pltpu.VMEM(wk.shape, bf16), pltpu.VMEM(wv.shape, bf16),
                         pltpu.VMEM(keys.shape, bf16), pltpu.VMEM(values.shape, bf16), pltpu.VMEM(wo.shape, bf16),
                         pltpu.VMEM(wg.shape, bf16), pltpu.VMEM(wu.shape, bf16), pltpu.VMEM(wd.shape, bf16), pltpu.VMEM(wqc.shape, bf16),
-                        pltpu.VMEM((batch, feat), f32), pltpu.VMEM((group, batch, feat), f32), pltpu.VMEM((batch, feat), f32), pltpu.VMEM((batch, feat), f32),
+                        pltpu.VMEM((batch, feat), f32), pltpu.VMEM((group, batch, feat), f32),
                         pltpu.VMEM((batch * 8, feat), f32)] + [pltpu.VMEM((2, mine * 8, feat), f32)] * 3
                        + [pltpu.VMEM((group + 1, mine, feat), f32)] * 2
                        + [pltpu.VMEM((mine, group * feat), bf16), pltpu.VMEM((mine, width), bf16), pltpu.VMEM((mine, ff), bf16)]
                        + [pltpu.VMEM((2, CHUNKS, 2, mine, chunk), f32)] + [pltpu.VMEM(chunk_shape, f32)] * 3 + [pltpu.VMEM((2, CHUNKS, 2, mine, chunk), f32)]
                        + [pltpu.VMEM((group, mine, feat), f32)] * 2
-                       + [pltpu.SemaphoreType.DMA((7,)), pltpu.SemaphoreType.DMA((loads,)), pltpu.SemaphoreType.DMA((loads,)), pltpu.SemaphoreType.DMA((2 * group,)),
+                       + [pltpu.SemaphoreType.DMA((6,)), pltpu.SemaphoreType.DMA((7,)), pltpu.SemaphoreType.DMA((loads,)), pltpu.SemaphoreType.DMA((loads,)), pltpu.SemaphoreType.DMA((2 * group,)),
                           pltpu.SemaphoreType.DMA((2, 2, 3, CHUNKS)), pltpu.SemaphoreType.DMA((2, 2))],
-        compiler_params=pltpu.CompilerParams(vmem_limit_bytes=BIG_VMEM, collective_id=1, has_side_effects=True),
+        compiler_params=pltpu.CompilerParams(vmem_limit_bytes=53 * 1024 * 1024, collective_id=1, has_side_effects=True),
         cost_estimate=pl.CostEstimate(flops=2 * batch * width * (3 * ff + 3 * qcols), bytes_accessed=50 * 1024 * 1024, transcendentals=batch * 8 * slots),
         name='self_layer',
-    )(seq_len, x, gains, keys, values, wq, wk, wv, wo, wg, wu, wd, wqc)
-
-
-def cross_tail(outs_in, tops_in, totals_in, hidden_in, tile_rows, gates, gains, wo, wg, wu, wd, group):
+    )(seq_len, *in_hbm(x, *gains, freqs, keys, values, wq, wk, wv, wo, wg, wu, wd, wqc))
+
+
+def cross_tail(packed, hidden_in, tile_rows, gates, gain, wo, wg, wu, wd, group):
     mine = hidden_in.shape[1]
-    feat = outs_in.shape[2]
+    feat = packed.shape[3]
     head_dim = feat // 2
     width, ff = wg.shape
     tiles = tile_rows.shape[0]
     chunk = width // CHUNKS // 2
 
-    def kernel(tile_ref, gate_ref, o_ref, m_ref, l_ref, h_ref, gains_ref, wo_hbm, wg_hbm, wu_hbm, wd_hbm, out_ref,
-               wo_ref, wg_ref, wu_ref, wd_ref, on_ref, h3_ref, tx, rx, att_ref, u_ref, act_ref,
-               part, from_core, chip, from_chip, total, final,
-               wsem, osem, red_sems, pair_sems, far_sems):
+    def kernel(tile_ref, gate_ref, p_ref, h_ref, gain_hbm, wo_hbm, wg_hbm, wu_hbm, wd_hbm, final,
+               gain_ref, wo_ref, wg_ref, wu_ref, wd_ref, on_ref, h3_ref, rx, att_ref, u_ref, act_ref,
+               part, from_core, chip, from_chip, total,
+               gsem, wsem, osem, red_sems, pair_sems, far_sems):
         row, core, other_core, other_chip, other_row = neighbours()
         barrier = pltpu.get_barrier_semaphore()
         greet(barrier, (other_core, other_chip, other_row))
         c_o = load_projection(wo_hbm, wo_ref, osem, group, head_dim)
-        for copy in c_o:
+        c_gain = pltpu.make_async_copy(gain_hbm, gain_ref, gsem)
+        for copy in c_o + [c_gain]:
             copy.start()
         c_w = [pltpu.make_async_copy(src, dst, wsem.at[i]) for i, (src, dst) in enumerate(((wg_hbm, wg_ref), (wu_hbm, wu_ref), (wd_hbm, wd_ref)))]
         for copy in c_w:
             copy.start()
-        pack_partial(tx, *(load_groups(ref, 1 - row, mine, feat, group) for ref in (o_ref, m_ref, l_ref)))
         pl.semaphore_wait(barrier, 3)
-        sent = remote(tx, rx, pair_sems, (0,), other_row)
+        sent = remote(p_ref.at[1 - row], rx, pair_sems, (0,), other_row)
         sent.start()
         for r in range(mine):
             seen = tile_ref[0, row * mine + r]
@@ -401,13 +425,13 @@
             on_ref[r:r + 1, :] = jnp.full((1, chunk), jnp.where(seen != 0, 1.0, 0.0))
         gate_att = jnp.tanh(jnp.full((1, chunk), gate_ref[0]))
         gate_mlp = jnp.tanh(jnp.full((1, chunk), gate_ref[1]))
-        outs, tops, counts = (load_groups(ref, row, mine, feat, group) for ref in (o_ref, m_ref, l_ref))
+        outs, tops, counts = unpack_partial(p_ref.at[row], group)
         sent.wait_recv()
         outs_p, tops_p, counts_p = unpack_partial(rx, group)
         for g in range(group):
             merged = merge(((outs[g], tops[g], counts[g]), (outs_p[g], tops_p[g], counts_p[g])))
             att_ref[:, g * feat:(g + 1) * feat] = merged.astype(jnp.bfloat16)
-        for copy in c_o:
+        for copy in c_o + [c_gain]:
             copy.wait()
         pending = [sent]
         ends = (core, other_core, other_chip)
@@ -415,7 +439,7 @@
         hidden = [(h_ref[k] + gate_att * on_ref[...] * total[k // 2, k % 2]).astype(jnp.bfloat16).astype(jnp.float32) for k in range(2 * CHUNKS)]
         for k in range(2 * CHUNKS):
             h3_ref[k] = hidden[k]
-        u_ref[...] = norm_chunks(hidden, gains_ref, 3)
+        u_ref[...] = norm_chunks(hidden, gain_ref)
         c_w[0].wait()
         c_w[1].wait()
         swiglu_hidden(u_ref, wg_ref, wu_ref, act_ref)
@@ -426,24 +450,23 @@
         for j in range(CHUNKS):
             second[j].wait_recv()
             summed = chip[1, j] + from_chip[1, j]
-            final[row, 2 * j + core] = (h3_ref[2 * j + core] + gate_mlp * on_ref[...] * summed).astype(jnp.bfloat16).astype(jnp.float32)
-            piece = final.at[row, 2 * j + core]
+            place = (pl.ds(pl.multiple_of(row * mine, mine), mine), pl.ds(pl.multiple_of((2 * j + core) * chunk, chunk), chunk))
+            final[place] = (h3_ref[2 * j + core] + gate_mlp * on_ref[...] * summed).astype(jnp.bfloat16).astype(jnp.float32)
+            piece = final.at[place]
             far.append(remote(piece, piece, far_sems, (0, j), other_row))
             far[j].start()
             near.append(remote(piece, piece, far_sems, (1, j), other_core))
             near[j].start()
         for j in range(CHUNKS):
             far[j].wait_recv()
-            piece = final.at[1 - row, 2 * j + core]
+            place = (pl.ds(pl.multiple_of((1 - row) * mine, mine), mine), pl.ds(pl.multiple_of((2 * j + core) * chunk, chunk), chunk))
+            piece = final.at[place]
             relay.append(remote(piece, piece, far_sems, (2, j), other_core))
             relay[j].start()
         for j in range(CHUNKS):
             near[j].wait_recv()
         for j in range(CHUNKS):
             relay[j].wait_recv()
-        for half in range(2):
-            for k in range(2 * CHUNKS):
-                out_ref[half * mine:(half + 1) * mine, k * chunk:(k + 1) * chunk] = final[half, k].astype(jnp.bfloat16)
         for copy in pending + near + far + relay:
             copy.wait_send()
 
@@ -451,109 +474,109 @@
     chunk_shape = (2, CHUNKS, mine, chunk)
     return pl.pallas_call(
         kernel,
-        out_shape=jax.ShapeDtypeStruct((2 * mine, width), bf16),
-        in_specs=[SMEM, SMEM] + [VMEM] * 5 + [ANY] * 4,
+        out_shape=jax.ShapeDtypeStruct((2 * mine, width), f32),
+        in_specs=[SMEM, SMEM] + [VMEM] * 2 + [ANY] * 5,
         out_specs=VMEM,
-        scratch_shapes=[pltpu.VMEM(wo.shape, bf16), pltpu.VMEM(wg.shape, bf16), pltpu.VMEM(wu.shape, bf16), pltpu.VMEM(wd.shape, bf16),
+        scratch_shapes=[pltpu.VMEM(gain.shape, bf16), pltpu.VMEM(wo.shape, bf16), pltpu.VMEM(wg.shape, bf16), pltpu.VMEM(wu.shape, bf16), pltpu.VMEM(wd.shape, bf16),
                         pltpu.VMEM((mine, chunk), f32), pltpu.VMEM((2 * CHUNKS, mine, chunk), f32)]
-                       + [pltpu.VMEM((group + 1, mine, feat), f32)] * 2
+                       + [pltpu.VMEM((group + 1, mine, feat), f32)]
                        + [pltpu.VMEM((mine, group * feat), bf16), pltpu.VMEM((mine, width), bf16), pltpu.VMEM((mine, ff), bf16)]
                        + [pltpu.VMEM((2, CHUNKS, 2, mine, chunk), f32)] + [pltpu.VMEM(chunk_shape, f32)] * 3 + [pltpu.VMEM((CHUNKS, 2, mine, chunk), f32)]
-                       + [pltpu.VMEM((2, 2 * CHUNKS, mine, chunk), f32)]
-                       + [pltpu.SemaphoreType.DMA((3,)), pltpu.SemaphoreType.DMA((2 * group,)),
+                       + [pltpu.SemaphoreType.DMA, pltpu.SemaphoreType.DMA((3,)), pltpu.SemaphoreType.DMA((2 * group,)),
                           pltpu.SemaphoreType.DMA((2, 2, 3, CHUNKS)), pltpu.SemaphoreType.DMA((2, 1)), pltpu.SemaphoreType.DMA((2, 3, CHUNKS))],
-        compiler_params=pltpu.CompilerParams(vmem_limit_bytes=BIG_VMEM, collective_id=2, has_side_effects=True),
+        compiler_params=pltpu.CompilerParams(vmem_limit_bytes=36 * 1024 * 1024, collective_id=2, has_side_effects=True),
         cost_estimate=pl.CostEstimate(flops=4 * mine * width * 3 * ff, bytes_accessed=30 * 1024 * 1024, transcendentals=mine * ff),
         name='cross_tail',
-    )(tile_rows, gates, outs_in, tops_in, totals_in, hidden_in, gains, wo, wg, wu, wd)
-
-
-def cross_attention(query_bd, keys, values, tile_rows):
+    )(tile_rows, gates, packed, hidden_in, *in_hbm(gain, wo, wg, wu, wd))
+
+
+def cross_attention(query_bd, keys, values, tile_rows, key_new, val_new):
     rows, feat, tokens = keys.shape
     tiles = tile_rows.shape[0]
-    half_tokens = tokens
-    tile_tok = half_tokens // 2
+    half_rows = rows // 2
+    head_dim = feat // 2
+    tile_tok = tokens // 2
     base_one = tile_tok // LANES * LANES
     width = tokens - base_one
-    width_pad = width
-    width_zero = min(width_pad, -(-tile_tok // LANES) * LANES)
-
-    def kernel(tile_ref, q_ref, k_hbm, v_hbm, o_ref, m_ref, l_ref, list_ref, kbuf, vbuf, ksem, vsem):
+    width_zero = min(width, -(-tile_tok // LANES) * LANES)
+
+    def kernel(tile_ref, q_ref, kin_ref, vin_ref, k_hbm, v_hbm, p_ref, kn_ref, vn_ref,
+               list_ref, o_ref, m_ref, l_ref, s_ref, kbuf, vbuf, ksem, vsem):
         kv_index = lax.axis_index('kv')
         first_tile = kv_index * (tiles // 2)
 
-        def add_zero(row, count):
-            list_ref[count] = row
-            return count + jnp.where(tile_ref[first_tile, row] != 0, 1, 0)
-
-        def add_one(row, count):
-            list_ref[count] = row
-            return count + jnp.where(tile_ref[first_tile + 1, row] != 0, 1, 0)
-
-        n_zero = lax.fori_loop(0, rows, add_zero, jnp.int32(0))
-        list_ref[n_zero] = list_ref[jnp.maximum(n_zero - 1, 0)]
-        pairs_zero = (n_zero + 1) // 2
-        start_one = 2 * pairs_zero
-        end_one = lax.fori_loop(0, rows, add_one, start_one)
-        n_one = end_one - start_one
-        list_ref[end_one] = list_ref[jnp.maximum(end_one - 1, 0)]
-        pairs = pairs_zero + (n_one + 1) // 2
-
-        def copies(index, is_one):
+        def collect(tile, count):
+            def add(row, count):
+                list_ref[count] = row
+                return count + jnp.where(tile_ref[first_tile + tile, row] != 0, 1, 0)
+
+            end = lax.fori_loop(0, rows, add, count, unroll=8)
+            list_ref[end] = list_ref[jnp.maximum(end - 1, 0)]
+            return end
+
+        def copies(index, is_one, hbm, buf, sem):
             slot = lax.rem(index, SLOTS)
-            out = []
-            for half in range(2):
-                row = list_ref[2 * index + half]
-                span = pl.ds(base_one, width) if is_one else pl.ds(0, width_zero)
-                dest = pl.ds(0, width) if is_one else pl.ds(0, width_zero)
-                for hbm, buf, sem in ((k_hbm, kbuf, ksem), (v_hbm, vbuf, vsem)):
-                    out.append(pltpu.make_async_copy(
-                        hbm.at[row, :, span], buf.at[slot, pl.ds(half * feat, feat), dest], sem.at[slot, half]))
-            return out
-
-        def start(index):
+            span = pl.ds(base_one, width) if is_one else pl.ds(0, width_zero)
+            dest = pl.ds(0, width) if is_one else pl.ds(0, width_zero)
+            return [pltpu.make_async_copy(hbm.at[list_ref[2 * index + half], :, span], buf.at[slot, pl.ds(half * feat, feat), dest], sem.at[slot, half])
+                    for half in range(2)]
+
+        key_side, val_side = (k_hbm, kbuf, ksem), (v_hbm, vbuf, vsem)
+
+        def start(index, is_one):
+            for copy in copies(index, is_one, *key_side) + copies(index, is_one, *val_side):
+                copy.start()
+
+        def wait(index, side):
             @pl.when(index < pairs_zero)
             def _():
-                for copy in copies(index, False):
-                    copy.start()
+                for copy in copies(index, False, *side):
+                    copy.wait()
 
             @pl.when((index >= pairs_zero) & (index < pairs))
             def _():
-                for copy in copies(index, True):
-                    copy.start()
-
-        def wait(index):
-            @pl.when(index < pairs_zero)
-            def _():
-                for copy in copies(index, False):
+                for copy in copies(index, True, *side):
                     copy.wait()
 
-            @pl.when(index >= pairs_zero)
-            def _():
-                for copy in copies(index, True):
-                    copy.wait()
-
+        n_zero = collect(0, jnp.int32(0))
+        pairs_zero = (n_zero + 1) // 2
         for index in range(SLOTS - 1):
-            start(jnp.int32(index))
+            pl.when(index < pairs_zero)(functools.partial(start, jnp.int32(index), False))
+        end_one = collect(1, 2 * pairs_zero)
+        pairs = (end_one + 1) // 2
+        for index in range(SLOTS - 1):
+            pl.when((index >= pairs_zero) & (index < pairs))(functools.partial(start, jnp.int32(index), True))
         o_ref[...] = jnp.zeros_like(o_ref)
         l_ref[...] = jnp.zeros_like(l_ref)
         m_ref[...] = jnp.full_like(m_ref, MASK_VALUE)
+        for src, dst in ((kin_ref, kn_ref), (vin_ref, vn_ref)):
+            dst[...] = jnp.stack([src[:, :head_dim], src[:, head_dim:]], axis=1).astype(jnp.bfloat16)
+
+        def scores_of(index):
+            last = jnp.minimum(index, jnp.maximum(pairs - 1, 0))
+            q_a, q_b = (q_ref[pl.ds(pl.multiple_of(list_ref[2 * last + half] * 8, 8), 8), :] for half in range(2))
+            zero = jnp.zeros_like(q_a)
+            q_pair = jnp.concatenate([jnp.concatenate([q_a, zero], axis=1), jnp.concatenate([zero, q_b], axis=1)], axis=0).astype(jnp.bfloat16)
+            return jnp.dot(q_pair, kbuf[lax.rem(index, SLOTS)], preferred_element_type=jnp.float32)
+
+        @pl.when(pairs > 0)
+        def _():
+            wait(jnp.int32(0), key_side)
+            s_ref[0] = scores_of(jnp.int32(0))
 
         def step(index, carry):
-            start(index + SLOTS - 1)
-            wait(index)
+            ahead = index + SLOTS - 1
+            pl.when(ahead < pairs_zero)(functools.partial(start, ahead, False))
+            pl.when((ahead >= pairs_zero) & (ahead < pairs))(functools.partial(start, ahead, True))
+            wait(index + 1, key_side)
+            wait(index, val_side)
             slot = lax.rem(index, SLOTS)
-            row_a = list_ref[2 * index]
-            row_b = list_ref[2 * index + 1]
             is_one = index >= pairs_zero
             low = jnp.where(is_one, tile_tok - base_one, 0)
             high = jnp.where(is_one, width, tile_tok)
-            high_b = jnp.where(is_one, jnp.where(2 * index + 1 == end_one, 0, high), jnp.where(2 * index + 1 == n_zero, 0, high))
-            q_a = q_ref[pl.ds(pl.multiple_of(row_a * 8, 8), 8), :]
-            q_b = q_ref[pl.ds(pl.multiple_of(row_b * 8, 8), 8), :]
-            zero = jnp.zeros_like(q_a)
-            q_pair = jnp.concatenate([jnp.concatenate([q_a, zero], axis=1), jnp.concatenate([zero, q_b], axis=1)], axis=0).astype(jnp.bfloat16)
-            scores = jnp.dot(q_pair, kbuf[slot], preferred_element_type=jnp.float32)
+            end = jnp.where(is_one, end_one, n_zero)
+            high_b = jnp.where(2 * index + 1 == end, 0, high)
+            scores = s_ref[lax.rem(index, 2)]
             lane = lax.broadcasted_iota(jnp.int32, scores.shape, 1)
             sub = lax.broadcasted_iota(jnp.int32, scores.shape, 0)
             visible = (lane >= low) & (lane < jnp.where(sub < 8, high, high_b))
@@ -561,12 +584,13 @@
             top = jnp.max(scores, axis=1, keepdims=True)
             probs = jnp.where(visible, jnp.exp((scores - top) * SCALE), 0.0)
             total = jnp.sum(probs, axis=1, keepdims=True)
+            following = scores_of(index + 1)
             lane_v = lax.broadcasted_iota(jnp.int32, (2 * feat, width - width_zero), 1)
             tail = jnp.where(lane_v < jnp.where(is_one, width, 0), vbuf[slot, :, width_zero:], jnp.zeros((), jnp.bfloat16))
             vals = jnp.concatenate([vbuf[slot, :, :width_zero], tail], axis=1)
             out = lax.dot_general(probs.astype(jnp.bfloat16), vals, (((1,), (1,)), ((), ())), preferred_element_type=jnp.float32)
-            for half, row in ((0, row_a), (1, row_b)):
-                where = pl.ds(pl.multiple_of(row * 8, 8), 8)
+            for half in range(2):
+                where = pl.ds(pl.multiple_of(list_ref[2 * index + half] * 8, 8), 8)
                 part = out[8 * half:8 * half + 8, feat * half:feat * half + feat]
                 top_new = jnp.broadcast_to(top[8 * half:8 * half + 8] * SCALE, (8, feat))
                 total_new = jnp.broadcast_to(total[8 * half:8 * half + 8], (8, feat))
@@ -577,25 +601,34 @@
                 m_ref[where, :] = best
                 l_ref[where, :] = l_ref[where, :] * w_old + total_new * w_new
                 o_ref[where, :] = o_ref[where, :] * w_old + part * w_new
+            s_ref[lax.rem(index + 1, 2)] = following
             return carry
 
         lax.fori_loop(0, pairs, step, 0)
-
-    flat = jax.ShapeDtypeStruct((rows * 8, feat), jnp.float32)
+        low_half = half_lane((half_rows, feat))
+        for half in range(2):
+            def groups(ref):
+                at = half * half_rows * 8
+                return [jnp.where(low_half, ref[pl.ds(at + g, half_rows, stride=8), :], ref[pl.ds(at + 4 + g, half_rows, stride=8), :]) for g in range(4)]
+
+            pack_partial(p_ref.at[half], groups(o_ref), groups(m_ref), groups(l_ref))
+
+    state = pltpu.VMEM((rows * 8, feat), jnp.float32)
+    heads = jax.ShapeDtypeStruct((rows, 2, head_dim), jnp.bfloat16)
     return pl.pallas_call(
         kernel,
-        out_shape=(flat, flat, flat),
-        in_specs=[pl.BlockSpec(memory_space=pltpu.SMEM), pl.BlockSpec(memory_space=pltpu.VMEM),
-                  pl.BlockSpec(memory_space=pl.ANY), pl.BlockSpec(memory_space=pl.ANY)],
-        out_specs=(pl.BlockSpec(memory_space=pltpu.VMEM),) * 3,
-        scratch_shapes=[pltpu.SMEM((2 * rows + 8,), jnp.int32),
-                        pltpu.VMEM((SLOTS, 2 * feat, width_pad), jnp.bfloat16),
-                        pltpu.VMEM((SLOTS, 2 * feat, width_pad), jnp.bfloat16),
+        out_shape=(jax.ShapeDtypeStruct((2, 5, half_rows, feat), jnp.float32), heads, heads),
+        in_specs=[SMEM, VMEM, VMEM, VMEM, ANY, ANY],
+        out_specs=(VMEM,) * 3,
+        scratch_shapes=[pltpu.SMEM((2 * rows + 8,), jnp.int32), state, state, state,
+                        pltpu.VMEM((2, 16, width), jnp.float32),
+                        pltpu.VMEM((SLOTS, 2 * feat, width), jnp.bfloat16),
+                        pltpu.VMEM((SLOTS, 2 * feat, width), jnp.bfloat16),
                         pltpu.SemaphoreType.DMA((SLOTS, 2)), pltpu.SemaphoreType.DMA((SLOTS, 2))],
-        compiler_params=pltpu.CompilerParams(vmem_limit_bytes=40 * 1024 * 1024),
+        compiler_params=pltpu.CompilerParams(vmem_limit_bytes=24 * 1024 * 1024),
         cost_estimate=pl.CostEstimate(flops=4 * 8 * feat * tokens * rows, bytes_accessed=2 * feat * tokens * rows, transcendentals=8 * tokens * rows),
         name='cross_attention',
-    )(tile_rows, query_bd, keys, values)
+    )(tile_rows, query_bd.reshape(rows * 8, feat), key_new, val_new, *in_hbm(keys, values))
 
 
 def solution(mesh):
@@ -616,19 +649,21 @@
         feat = kv_local * head_dim
         group = wq_self.shape[1] // feat
         tokens = kx_cache.shape[2]
-        rows = [attn_norm, mlp_norm, xattn_norm, xmlp_norm, jnp.tile(q_norm, width // head_dim)]
-        gains = jnp.stack([r.astype(jnp.float32) for r in rows] + [jnp.tile(rope_freqs(head_dim), 2 * width // head_dim)] + [jnp.zeros((width,), jnp.float32)] * 2)
+        freqs = jnp.tile(rope_freqs(head_dim), 2 * feat // head_dim)[None]
+
+        def lane_rows(gain):
+            return gain.reshape(-1, LANES)
 
         def token_minor(cache):
             return jnp.swapaxes(cache, 2, 3).reshape(batch, feat, cache.shape[2])
 
         key_new, val_new, query_x, h_two = self_layer(
-            x, token_minor(ks_cache).reshape(batch * feat, slots), token_minor(vs_cache).reshape(batch * feat, slots), seq_len, gains,
+            x, token_minor(ks_cache).reshape(batch * feat, slots), token_minor(vs_cache).reshape(batch * feat, slots), seq_len,
+            [lane_rows(attn_norm), lane_rows(mlp_norm), lane_rows(xattn_norm), q_norm[None]], freqs,
             wq_self, wk_self, wv_self, wo_self, wg_self, wu_self, wd_self, wq_cross, group)
         tile_rows = tile_vis.T
-        parts = cross_attention(query_x.reshape(batch * 8, feat), token_minor(kx_cache), token_minor(vx_cache), tile_rows)
-        parts = [p.reshape(2, batch * 4, feat) for p in parts]
-        h_four = cross_tail(*parts, h_two, tile_rows, cross_gates, gains, wo_cross, wg_cross, wu_cross, wd_cross, group)
-        return h_four, key_new.reshape(batch, kv_local, head_dim), val_new.reshape(batch, kv_local, head_dim)
+        packed, key_new, val_new = cross_attention(query_x, token_minor(kx_cache), token_minor(vx_cache), tile_rows, key_new, val_new)
+        h_four = cross_tail(packed, h_two, tile_rows, cross_gates, lane_rows(xmlp_norm), wo_cross, wg_cross, wu_cross, wd_cross, group)
+        return h_four.astype(jnp.bfloat16), key_new, val_new
 
     return jax.shard_map(device_step, mesh=mesh, in_specs=in_specs, out_specs=out_specs, check_vma=False)

time: 114 us -> 92.1 us (0.81); the launches traced: 113 us -> 92.3 us
  Pallas kernels: 101 us -> 88.9 us
  local copies, waits for them, and re-layouts: 8.33 us -> 1.92 us
  other arithmetic: 2.75 us -> 0.73 us
    pallas_call x2, Pallas kernels: 70.5 us -> 60.4 us  [the longest x1 37.7 us: self_layer(): pl.pallas_call(kernel, out_shape=(jax.ShapeDtypeStruct((batch, feat), f32...]
    unnamed x15 -> x6, local copies, waits for them, and re-layouts: 4.73 us -> 0.66 us
    another operation x4 -> x0, other arithmetic: 2.75 us -> none  [device_step(): jnp.stack([r.astype(jnp.float32) for r in rows] + [jnp.tile(rope_freqs(he...]
    pallas_call x1, Pallas kernels: 30.5 us -> 28.5 us  [cross_tail(): pl.pallas_call(kernel, out_shape=jax.ShapeDtypeStruct((2 * mine, width),...]
    reshape x2 -> x0, local copies, waits for them, and re-layouts: 1.4 us -> none  [the longest x1 0.7 us: device_step(): key_new.reshape(batch, kv_local, head_dim)]
where the time goes in v1:
time: 92.1 us; the launch traced here: 92.3 us
  Pallas kernels  88.9 us (97%)
  local copies, waits for them, and re-layouts  1.92 us (2%)
    pallas_call x1, Pallas kernels, self_layer(): pl.pallas_call(kernel, out_shape=(jax.ShapeDtypeStruct((batch, feat), f32...  37.7 us
    pallas_call x1, Pallas kernels, cross_tail(): pl.pallas_call(kernel, out_shape=jax.ShapeDtypeStruct((2 * mine, width),...  28.5 us
    pallas_call x1, Pallas kernels, cross_attention(): pl.pallas_call(kernel, out_shape=(jax.ShapeDtypeStruct((2, 5, half_rows,...  22.7 us

profile of v1, /device:TPU:0, one launch (start us, length us, event | category | flops | bytes accessed | tf_op | source)
XLA Modules:
  0.0 92.3 jit_solution(16052075836485733049)
XLA Ops:
  0.6 0.7 tile.2
  1.3 0.6 broadcast_in_dim_tile.3.f_hbm
  1.9 0.0 copy-start.1
  1.9 0.7 copy-done.1
  2.5 0.0 copy-start
  2.5 37.7 %self_layer.1 = (f32[64,128]{1,0:T(8,128)S(1)}, f32[64,128]{1,0:T(8,128)S(1)}, f32[2,256,128]{2,1,0:T(8,128)S(1)}, f32[8,32,256]{2,1,0:T(8,128)S(1)}) custom-call(s32[64]{0:T(128)S(1)} %copy-done.1, bf16[64,2048]{1,0:T(8,128)(2,1)} %x_hbm.1, bf16[16,128]{1,0:T(8,128)(2,1)} %bitcast.26, bf16[16,128]{1,0:T(8,128)(2,1)} %bitcast.27, bf16[16,128]{1,0:T(8,128)(2,1)} %bitcast.28, ...), custom_call_target="tpu_custom_call" | custom-call | flops 2013265920 | bytes 52428800 | tf_op jit(solution)/shard_map/self_layer/pallas_call | solution.py:372
  40.3 0.0 copy-done
  40.3 0.0 copy-start.2
  40.3 22.7 %cross_attention.1 = (f32[2,5,32,128]{3,2,1,0:T(8,128)S(1)}, bf16[64,2,64]{2,1,0:T(2,128)(2,1)}, bf16[64,2,64]{2,1,0:T(2,128)(2,1)}) custom-call(s32[4,64]{1,0:T(4,128)S(1)} %bitcast.20, f32[512,128]{1,0:T(8,128)S(1)} %bitcast.19, f32[64,128]{1,0:T(8,128)S(1)} %get-tuple-element.11.kin_ref, f32[64,128]{1,0:T(8,128)S(1)} %get-tuple-element.12.vin_ref, ...), custom_call_target="tpu_custom_call" | custom-call | flops 839385088 | bytes 52461568 | tf_op jit(solution)/shard_map/cross_attention/pallas_call | solution.py:618
  63.0 0.0 copy-done.2
  63.0 28.5 %cross_tail.1 = f32[64,2048]{1,0:T(8,128)S(1)} custom-call(s32[4,64]{1,0:T(4,128)S(1)} %bitcast.21, f32[2]{0:T(128)S(1)} %copy-done.2, f32[2,5,32,128]{3,2,1,0:T(8,128)S(1)} %get-tuple-element.13.p_ref, f32[8,32,256]{2,1,0:T(8,128)S(1)} %get-tuple-element.14.h_ref, bf16[16,128]{1,0:T(8,128)(2,1)} %bitcast.29, bf16[512,2048]{1,0:T(8,128)(2,1)} %wo_hbm.3, ...), custom_call_target="tpu_custom_call" | custom-call | flops 1610612736 | bytes 31457280 | tf_op jit(solution)/shard_map/cross_tail/pallas_call | solution.py:475
  91.5 0.7 convert_element_type.3
Async XLA Ops:
  1.9 0.7 copy-start.1
  2.5 37.7 %copy-start = (s32[64,4]{0,1:T(4,128)S(1)}, s32[64,4]{0,1:T(4,128)}, u32[]{:S(2)}) copy-start(s32[64,4]{0,1:T(4,128)} %param.32) | copy-start | bytes 3076
  40.3 22.7 %copy-start.2 = (f32[2]{0:T(128)S(1)}, f32[2]{0:T(128)}, u32[]{:S(2)}) copy-start(f32[2]{0:T(128)} %gate_ref.1) | copy-start | bytes 28

commit v2 on v1

--- a/solution.py
+++ b/solution.py
@@ -2,6 +2,7 @@
 import math
 import jax
 import jax.numpy as jnp
+import numpy as np
 from jax import lax
 from jax.experimental import pallas as pl
 from jax.experimental.pallas import tpu as pltpu
@@ -11,7 +12,8 @@
 ROPE_THETA = 500000.0
 MASK_VALUE = -1e30
 LANES = 128
-SLOTS = 5
+SLOTS = 7
+AHEAD = 2
 SCALE = 0.125
 
 
@@ -27,11 +29,12 @@
         else:
             smooth = (8192.0 / wave_len - 1.0) / 3.0
             freq_list.append((1.0 - smooth) * base_freq / 8.0 + smooth * base_freq)
-    return jnp.array(freq_list, dtype=jnp.float32)
+    return np.array(freq_list, dtype=np.float32)
 
 
 MESH_ID = pl.DeviceIdType.MESH
 CHUNKS = 4
+LAST_CHUNKS = 4
 ANY = pl.BlockSpec(memory_space=pl.ANY)
 VMEM = pl.BlockSpec(memory_space=pltpu.VMEM)
 SMEM = pl.BlockSpec(memory_space=pltpu.SMEM)
@@ -61,7 +64,8 @@
 
 def reduce_chips(produce, part, from_core, chip, from_chip, sems, core, other_core, other_chip):
     first, second = [], []
-    for j in range(CHUNKS):
+    chunks = part.shape[0]
+    for j in range(chunks):
         block = produce(j)
         width = block.shape[1] // 2
         part[j, 0] = block[:, :width]
@@ -69,7 +73,7 @@
         copy = remote(part.at[j, 1 - core], from_core.at[j], sems, (0, j), other_core)
         copy.start()
         first.append(copy)
-    for j in range(CHUNKS):
+    for j in range(chunks):
         first[j].wait_recv()
         chip[j] = part[j, core] + from_core[j]
         copy = remote(chip.at[j], from_chip.at[j], sems, (1, j), other_chip)
@@ -78,17 +82,25 @@
     return first, second
 
 
-def all_reduce(produce, part, from_core, chip, from_chip, total, sems, core, other_core, other_chip):
+def all_reduce(produce, use, part, from_core, chip, from_chip, total, sems, core, other_core, other_chip):
     first, second = reduce_chips(produce, part, from_core, chip, from_chip, sems, core, other_core, other_chip)
+    chunks, width = part.shape[0], part.shape[3]
+
+    def column(j, half):
+        return pl.multiple_of((2 * j + half) * width, width)
+
     third = []
-    for j in range(CHUNKS):
+    for j in range(chunks):
         second[j].wait_recv()
         total[j, core] = chip[j] + from_chip[j]
-        copy = remote(total.at[j, core], total.at[j, core], sems, (2, j), other_core)
-        copy.start()
-        third.append(copy)
-    for copy in third:
-        copy.wait_recv()
+        third.append(remote(total.at[j, core], total.at[j, core], sems, (2, j), other_core))
+        third[j].start()
+        if j > 0:
+            third[j - 1].wait_recv()
+            use(column(j - 1, 1 - core), total[j - 1, 1 - core])
+        use(column(j, core), total[j, core])
+    third[-1].wait_recv()
+    use(column(chunks - 1, 1 - core), total[chunks - 1, 1 - core])
     return first + second + third
 
 
@@ -97,26 +109,39 @@
     return jnp.concatenate([gain[k:k + 1] for k in range(gain.shape[0])], axis=1)
 
 
-def norm_chunks(chunks, gain_ref):
-    width = chunks[0].shape[1]
-    gain = lane_row(gain_ref)
-    square = sum(jnp.sum(c * c, axis=1, keepdims=True) for c in chunks)
-    inv = lax.rsqrt(square / (width * len(chunks)) + NORM_EPS)
-    return jnp.concatenate([(c * inv * gain[:, k * width:(k + 1) * width]).astype(jnp.bfloat16)
-                            for k, c in enumerate(chunks)], axis=1)
-
-
-def swiglu_hidden(u_ref, wg_ref, wu_ref, act_ref):
+def norm_products(old_at, h_ref, square_ref, gain_ref, pairs):
+    square_ref[...] = jnp.zeros_like(square_ref)
+    for _, acc in pairs:
+        acc[...] = jnp.zeros_like(acc)
+
+    def use(column, summed):
+        width = summed.shape[1]
+        cols = pl.ds(column, width)
+        hidden = (old_at(cols, summed)).astype(jnp.bfloat16).astype(jnp.float32)
+        h_ref[:, cols] = hidden
+        square_ref[...] += jnp.sum(hidden * hidden, axis=1, keepdims=True)
+        scaled = (hidden * gain_ref[:, cols]).astype(jnp.bfloat16)
+        for w_ref, acc in pairs:
+            block = min(512, acc.shape[1])
+            for n in range(0, acc.shape[1], block):
+                acc[:, n:n + block] += jnp.dot(scaled, w_ref[cols, n:n + block], preferred_element_type=jnp.float32)
+
+    return use
+
+
+def norm_scale(square_ref, width):
+    return lax.rsqrt(square_ref[:, :1] / width + NORM_EPS)
+
+
+def swiglu_hidden(inv, gate_ref, upper_ref, act_ref):
     block = 512
-    for n in range(wg_ref.shape[1] // block):
-        cols = pl.ds(n * block, block)
-        gate = jnp.dot(u_ref[...], wg_ref[:, cols], preferred_element_type=jnp.float32)
-        upper = jnp.dot(u_ref[...], wu_ref[:, cols], preferred_element_type=jnp.float32)
-        act_ref[:, cols] = (jax.nn.silu(gate) * upper).astype(jnp.bfloat16)
-
-
-def chunk_dot(lhs_ref, w_ref):
-    block = w_ref.shape[1] // CHUNKS
+    for n in range(0, act_ref.shape[1], block):
+        cols = slice(n, n + block)
+        act_ref[:, cols] = (jax.nn.silu(gate_ref[:, cols] * inv) * (upper_ref[:, cols] * inv)).astype(jnp.bfloat16)
+
+
+def chunk_dot(lhs_ref, w_ref, chunks):
+    block = w_ref.shape[1] // chunks
     return lambda j: jnp.dot(lhs_ref[...], w_ref[:, j * block:(j + 1) * block], preferred_element_type=jnp.float32)
 
 
@@ -209,10 +234,10 @@
     loads = batch // GROUP_ROWS
     chunk = width // CHUNKS // 2
 
-    def kernel(seq_ref, x_hbm, ga_hbm, gm_hbm, gx_hbm, gq_hbm, f_hbm, k_hbm, v_hbm, wq_hbm, wk_hbm, wv_hbm, wo_hbm, wg_hbm, wu_hbm, wd_hbm, wqc_hbm,
+    def kernel(seq_hbm, x_hbm, ga_hbm, gm_hbm, gx_hbm, gq_hbm, f_hbm, k_hbm, v_hbm, wq_hbm, wk_hbm, wv_hbm, wo_hbm, wg_hbm, wu_hbm, wd_hbm, wqc_hbm,
                kn_ref, vn_ref, qx_ref, h_ref,
-               x_ref, ga_ref, gm_ref, gx_ref, gq_ref, f_ref, wq_ref, wk_ref, wv_ref, kbuf, vbuf, wo_ref, wg_ref, wu_ref, wd_ref, wqc_ref,
-               seqf, qg_ref, q3_ref, o_ref, m_ref, l_ref, tx, rx, att_ref, u_ref, act_ref,
+               seq_ref, x_ref, ga_ref, gm_ref, gx_ref, gq_ref, f_ref, wq_ref, wk_ref, wv_ref, kbuf, vbuf, wo_ref, wg_ref, wu_ref, wd_ref, wqc_ref,
+               seqf, qg_ref, q3_ref, o_ref, m_ref, l_ref, tx, rx, att_ref, gm_row, gx_row, square, gate_acc, upper_acc, query_acc, act_ref,
                part, from_core, chip, from_chip, total, qtx, qrx,
                xsem, wsem, ksem, vsem, osem, red_sems, pair_sems):
         row, core, other_core, other_chip, other_row = neighbours()
@@ -220,7 +245,7 @@
         greet(barrier, (other_core, other_chip, other_row))
 
         small = [pltpu.make_async_copy(src, dst, xsem.at[i]) for i, (src, dst) in enumerate(
-            ((f_hbm, f_ref), (ga_hbm, ga_ref), (x_hbm, x_ref), (gm_hbm, gm_ref), (gx_hbm, gx_ref), (gq_hbm, gq_ref)))]
+            ((seq_hbm, seq_ref), (f_hbm, f_ref), (ga_hbm, ga_ref), (x_hbm, x_ref), (gm_hbm, gm_ref), (gx_hbm, gx_ref), (gq_hbm, gq_ref)))]
         for copy in small:
             copy.start()
 
@@ -246,10 +271,12 @@
         c_g, c_u, c_d, c_qc = (pltpu.make_async_copy(src, dst, wsem.at[3 + i]) for i, (src, dst) in enumerate(
             ((wg_hbm, wg_ref), (wu_hbm, wu_ref), (wd_hbm, wd_ref), (wqc_hbm, wqc_ref))))
         start_cache(0)
+        for copy in small:
+            copy.wait()
         for b in range(batch):
             seqf[b:b + 1, :] = jnp.full((1, feat), seq_ref[b].astype(jnp.float32))
-        for copy in small:
-            copy.wait()
+        gm_row[...] = lane_row(gm_ref)
+        gx_row[...] = lane_row(gx_ref)
         angles = seqf[...] * f_ref[...]
         lane = lax.rem(lax.broadcasted_iota(jnp.int32, (batch, feat), 1), head_dim)
         first = lane < head_dim // 2
@@ -277,21 +304,26 @@
         kn_ref[...] = key_new
         vn_ref[...] = val_new.astype(jnp.float32)
 
-        def attend(phase, start, local):
+        def scores_of(start):
             q_a = q3_ref[pl.ds(pl.multiple_of(start * 8, 16), 8), :]
             q_b = q3_ref[pl.ds(pl.multiple_of(start * 8, 16) + 8, 8), :]
             zero = jnp.zeros_like(q_a)
             q_pair = jnp.concatenate([jnp.concatenate([q_a, zero], axis=1), jnp.concatenate([zero, q_b], axis=1)], axis=0).astype(jnp.bfloat16)
             rows = pl.ds(pl.multiple_of(start * feat, 2 * feat), 2 * feat)
-            scores = jnp.dot(q_pair, kbuf[rows, :], preferred_element_type=jnp.float32)
+            return jnp.dot(q_pair, kbuf[rows, :], preferred_element_type=jnp.float32)
+
+        def probs_of(scores, start):
             slot = lax.broadcasted_iota(jnp.int32, scores.shape, 1)
             sub = lax.broadcasted_iota(jnp.int32, scores.shape, 0)
             visible = slot < jnp.where(sub < 8, seq_ref[start], seq_ref[start + 1]) - row * slots
             scores = jnp.where(visible, scores, MASK_VALUE)
             top = jnp.max(scores, axis=1, keepdims=True)
             probs = jnp.where(visible, jnp.exp((scores - top) * SCALE), 0.0)
-            count = jnp.sum(probs, axis=1, keepdims=True)
-            out = lax.dot_general(probs.astype(jnp.bfloat16), vbuf[rows, :], (((1,), (1,)), ((), ())), preferred_element_type=jnp.float32)
+            return probs.astype(jnp.bfloat16), top, jnp.sum(probs, axis=1, keepdims=True)
+
+        def weigh(probs, top, count, phase, start, local):
+            rows = pl.ds(pl.multiple_of(start * feat, 2 * feat), 2 * feat)
+            out = lax.dot_general(probs, vbuf[rows, :], (((1,), (1,)), ((), ())), preferred_element_type=jnp.float32)
             for half in range(2):
                 where = pl.ds(local * 8 + 8 * half, 8)
                 o_ref[phase, where, :] = out[8 * half:8 * half + 8, feat * half:feat * half + feat]
@@ -305,9 +337,13 @@
             following()
             phase, part_rows = quarter // 2, mine // 2
             start = lax.rem((1 + phase - row) * mine, batch)
-            for p in range(part_rows // 2):
-                local = (quarter % 2) * part_rows + 2 * p
-                attend(phase, start + local, local)
+            places = [(quarter % 2) * part_rows + 2 * p for p in range(part_rows // 2)]
+            scores = [scores_of(start + local) for local in places[:AHEAD]]
+            for p, local in enumerate(places):
+                soft = probs_of(scores[p], start + local)
+                if p + AHEAD < len(places):
+                    scores.append(scores_of(start + places[p + AHEAD]))
+                weigh(*soft, phase, start + local, local)
 
         def start_all(*copies):
             for copy in copies:
@@ -336,23 +372,16 @@
             copy.wait()
         pending = [sent]
         ends = (core, other_core, other_chip)
-        pending += all_reduce(chunk_dot(att_ref, wo_ref), part.at[0], from_core.at[0], chip.at[0], from_chip.at[0], total.at[0], red_sems.at[0], *ends)
-        cols = [slice(k * chunk, (k + 1) * chunk) for k in range(2 * CHUNKS)]
-        hidden = [(x_ref[own, cols[k]].astype(jnp.float32) + total[0, k // 2, k % 2]).astype(jnp.bfloat16).astype(jnp.float32) for k in range(2 * CHUNKS)]
-        for k in range(2 * CHUNKS):
-            h_ref[k] = hidden[k]
-        u_ref[...] = norm_chunks(hidden, gm_ref)
         c_g.wait()
         c_u.wait()
-        swiglu_hidden(u_ref, wg_ref, wu_ref, act_ref)
+        use = norm_products(lambda cols, summed: x_ref[own, cols].astype(jnp.float32) + summed, h_ref, square, gm_row, ((wg_ref, gate_acc), (wu_ref, upper_acc)))
+        pending += all_reduce(chunk_dot(att_ref, wo_ref, CHUNKS), use, part.at[0], from_core.at[0], chip.at[0], from_chip.at[0], total.at[0], red_sems.at[0], *ends)
+        swiglu_hidden(norm_scale(square, width), gate_acc, upper_acc, act_ref)
         c_d.wait()
-        pending += all_reduce(chunk_dot(act_ref, wd_ref), part.at[1], from_core.at[1], chip.at[1], from_chip.at[1], total.at[1], red_sems.at[1], *ends)
-        hidden = [(h_ref[k] + total[1, k // 2, k % 2]).astype(jnp.bfloat16).astype(jnp.float32) for k in range(2 * CHUNKS)]
-        for k in range(2 * CHUNKS):
-            h_ref[k] = hidden[k]
-        u_ref[...] = norm_chunks(hidden, gx_ref)
         c_qc.wait()
-        query = jnp.dot(u_ref[...], wqc_ref[...], preferred_element_type=jnp.float32)
+        use = norm_products(lambda cols, summed: h_ref[:, cols] + summed, h_ref, square, gx_row, ((wqc_ref, query_acc),))
+        pending += all_reduce(chunk_dot(act_ref, wd_ref, CHUNKS), use, part.at[1], from_core.at[1], chip.at[1], from_chip.at[1], total.at[1], red_sems.at[1], *ends)
+        query = query_acc[...] * norm_scale(square, width)
         groups = by_group([query[:, n * feat:(n + 1) * feat] for n in range(qcols // feat)], group)
         gain = jnp.concatenate([gq_ref[...].astype(jnp.float32)] * 2, axis=1)
         groups = [(v * lax.rsqrt(half_sums(v * v) / head_dim + NORM_EPS) * gain).astype(jnp.bfloat16).astype(jnp.float32) for v in groups]
@@ -372,45 +401,47 @@
     return pl.pallas_call(
         kernel,
         out_shape=(jax.ShapeDtypeStruct((batch, feat), f32), jax.ShapeDtypeStruct((batch, feat), f32),
-                   jax.ShapeDtypeStruct((2, mine * 8, feat), f32), jax.ShapeDtypeStruct((2 * CHUNKS, mine, chunk), f32)),
-        in_specs=[SMEM] + [ANY] * 16,
+                   jax.ShapeDtypeStruct((2, mine * 8, feat), f32), jax.ShapeDtypeStruct((mine, width), f32)),
+        in_specs=[ANY] * 17,
         out_specs=(VMEM,) * 4,
-        scratch_shapes=[pltpu.VMEM(a.shape, a.dtype) for a in (x, *gains, freqs)]
+        scratch_shapes=[pltpu.SMEM(seq_len.shape, seq_len.dtype)] + [pltpu.VMEM(a.shape, a.dtype) for a in (x, *gains, freqs)]
                        + [pltpu.VMEM(wq.shape, bf16), pltpu.VMEM(wk.shape, bf16), pltpu.VMEM(wv.shape, bf16),
                         pltpu.VMEM(keys.shape, bf16), pltpu.VMEM(values.shape, bf16), pltpu.VMEM(wo.shape, bf16),
                         pltpu.VMEM(wg.shape, bf16), pltpu.VMEM(wu.shape, bf16), pltpu.VMEM(wd.shape, bf16), pltpu.VMEM(wqc.shape, bf16),
                         pltpu.VMEM((batch, feat), f32), pltpu.VMEM((group, batch, feat), f32),
                         pltpu.VMEM((batch * 8, feat), f32)] + [pltpu.VMEM((2, mine * 8, feat), f32)] * 3
                        + [pltpu.VMEM((group + 1, mine, feat), f32)] * 2
-                       + [pltpu.VMEM((mine, group * feat), bf16), pltpu.VMEM((mine, width), bf16), pltpu.VMEM((mine, ff), bf16)]
+                       + [pltpu.VMEM((mine, group * feat), bf16), pltpu.VMEM((1, width), f32), pltpu.VMEM((1, width), f32), pltpu.VMEM((mine, LANES), f32),
+                          pltpu.VMEM((mine, ff), f32), pltpu.VMEM((mine, ff), f32), pltpu.VMEM((mine, qcols), f32), pltpu.VMEM((mine, ff), bf16)]
                        + [pltpu.VMEM((2, CHUNKS, 2, mine, chunk), f32)] + [pltpu.VMEM(chunk_shape, f32)] * 3 + [pltpu.VMEM((2, CHUNKS, 2, mine, chunk), f32)]
                        + [pltpu.VMEM((group, mine, feat), f32)] * 2
-                       + [pltpu.SemaphoreType.DMA((6,)), pltpu.SemaphoreType.DMA((7,)), pltpu.SemaphoreType.DMA((loads,)), pltpu.SemaphoreType.DMA((loads,)), pltpu.SemaphoreType.DMA((2 * group,)),
+                       + [pltpu.SemaphoreType.DMA((7,)), pltpu.SemaphoreType.DMA((7,)), pltpu.SemaphoreType.DMA((loads,)), pltpu.SemaphoreType.DMA((loads,)), pltpu.SemaphoreType.DMA((2 * group,)),
                           pltpu.SemaphoreType.DMA((2, 2, 3, CHUNKS)), pltpu.SemaphoreType.DMA((2, 2))],
         compiler_params=pltpu.CompilerParams(vmem_limit_bytes=53 * 1024 * 1024, collective_id=1, has_side_effects=True),
         cost_estimate=pl.CostEstimate(flops=2 * batch * width * (3 * ff + 3 * qcols), bytes_accessed=50 * 1024 * 1024, transcendentals=batch * 8 * slots),
         name='self_layer',
-    )(seq_len, *in_hbm(x, *gains, freqs, keys, values, wq, wk, wv, wo, wg, wu, wd, wqc))
+    )(*in_hbm(seq_len, x, *gains, freqs, keys, values, wq, wk, wv, wo, wg, wu, wd, wqc))
 
 
 def cross_tail(packed, hidden_in, tile_rows, gates, gain, wo, wg, wu, wd, group):
-    mine = hidden_in.shape[1]
+    mine = hidden_in.shape[0]
     feat = packed.shape[3]
     head_dim = feat // 2
     width, ff = wg.shape
     tiles = tile_rows.shape[0]
     chunk = width // CHUNKS // 2
-
-    def kernel(tile_ref, gate_ref, p_ref, h_ref, gain_hbm, wo_hbm, wg_hbm, wu_hbm, wd_hbm, final,
-               gain_ref, wo_ref, wg_ref, wu_ref, wd_ref, on_ref, h3_ref, rx, att_ref, u_ref, act_ref,
-               part, from_core, chip, from_chip, total,
-               gsem, wsem, osem, red_sems, pair_sems, far_sems):
+    last = width // LAST_CHUNKS // 2
+
+    def kernel(tile_hbm, gate_hbm, p_ref, h_ref, gain_hbm, wo_hbm, wg_hbm, wu_hbm, wd_hbm, final,
+               tile_ref, gate_ref, gain_ref, wo_ref, wg_ref, wu_ref, wd_ref, on_ref, h3_ref, rx, att_ref, gain_row, square, gate_acc, upper_acc, act_ref,
+               part, from_core, chip, from_chip, total, last_part, last_from_core, last_chip, last_from_chip,
+               gsem, wsem, osem, red_sems, last_sems, pair_sems, far_sems):
         row, core, other_core, other_chip, other_row = neighbours()
         barrier = pltpu.get_barrier_semaphore()
         greet(barrier, (other_core, other_chip, other_row))
         c_o = load_projection(wo_hbm, wo_ref, osem, group, head_dim)
-        c_gain = pltpu.make_async_copy(gain_hbm, gain_ref, gsem)
-        for copy in c_o + [c_gain]:
+        small = [pltpu.make_async_copy(src, dst, gsem.at[i]) for i, (src, dst) in enumerate(((tile_hbm, tile_ref), (gate_hbm, gate_ref), (gain_hbm, gain_ref)))]
+        for copy in small + c_o:
             copy.start()
         c_w = [pltpu.make_async_copy(src, dst, wsem.at[i]) for i, (src, dst) in enumerate(((wg_hbm, wg_ref), (wu_hbm, wu_ref), (wd_hbm, wd_ref)))]
         for copy in c_w:
@@ -418,76 +449,80 @@
         pl.semaphore_wait(barrier, 3)
         sent = remote(p_ref.at[1 - row], rx, pair_sems, (0,), other_row)
         sent.start()
+        for copy in small:
+            copy.wait()
+        gain_row[...] = lane_row(gain_ref)
         for r in range(mine):
             seen = tile_ref[0, row * mine + r]
             for t in range(1, tiles):
                 seen = jnp.maximum(seen, tile_ref[t, row * mine + r])
-            on_ref[r:r + 1, :] = jnp.full((1, chunk), jnp.where(seen != 0, 1.0, 0.0))
-        gate_att = jnp.tanh(jnp.full((1, chunk), gate_ref[0]))
-        gate_mlp = jnp.tanh(jnp.full((1, chunk), gate_ref[1]))
+            on_ref[r:r + 1, :] = jnp.full((1, LANES), jnp.where(seen != 0, 1.0, 0.0))
+        gate_att = jnp.tanh(jnp.full((1, LANES), gate_ref[0]))[:, :1]
+        gate_mlp = jnp.tanh(jnp.full((1, LANES), gate_ref[1]))[:, :1]
         outs, tops, counts = unpack_partial(p_ref.at[row], group)
         sent.wait_recv()
         outs_p, tops_p, counts_p = unpack_partial(rx, group)
         for g in range(group):
             merged = merge(((outs[g], tops[g], counts[g]), (outs_p[g], tops_p[g], counts_p[g])))
             att_ref[:, g * feat:(g + 1) * feat] = merged.astype(jnp.bfloat16)
-        for copy in c_o + [c_gain]:
+        for copy in c_o:
             copy.wait()
         pending = [sent]
         ends = (core, other_core, other_chip)
-        pending += all_reduce(chunk_dot(att_ref, wo_ref), part.at[0], from_core.at[0], chip.at[0], from_chip.at[0], total, red_sems.at[0], *ends)
-        hidden = [(h_ref[k] + gate_att * on_ref[...] * total[k // 2, k % 2]).astype(jnp.bfloat16).astype(jnp.float32) for k in range(2 * CHUNKS)]
-        for k in range(2 * CHUNKS):
-            h3_ref[k] = hidden[k]
-        u_ref[...] = norm_chunks(hidden, gain_ref)
         c_w[0].wait()
         c_w[1].wait()
-        swiglu_hidden(u_ref, wg_ref, wu_ref, act_ref)
+        scale_att, scale_mlp = gate_att * on_ref[:, :1], gate_mlp * on_ref[:, :1]
+        use = norm_products(lambda cols, summed: h_ref[:, cols] + scale_att * summed, h3_ref, square, gain_row, ((wg_ref, gate_acc), (wu_ref, upper_acc)))
+        pending += all_reduce(chunk_dot(att_ref, wo_ref, CHUNKS), use, part, from_core, chip, from_chip, total, red_sems, *ends)
+        swiglu_hidden(norm_scale(square, width), gate_acc, upper_acc, act_ref)
         c_w[2].wait()
-        first, second = reduce_chips(chunk_dot(act_ref, wd_ref), part.at[1], from_core.at[1], chip.at[1], from_chip.at[1], red_sems.at[1], *ends)
+        first, second = reduce_chips(chunk_dot(act_ref, wd_ref, LAST_CHUNKS), last_part, last_from_core, last_chip, last_from_chip, last_sems, *ends)
         pending += first + second
         near, far, relay = [], [], []
-        for j in range(CHUNKS):
+        for j in range(LAST_CHUNKS):
             second[j].wait_recv()
-            summed = chip[1, j] + from_chip[1, j]
-            place = (pl.ds(pl.multiple_of(row * mine, mine), mine), pl.ds(pl.multiple_of((2 * j + core) * chunk, chunk), chunk))
-            final[place] = (h3_ref[2 * j + core] + gate_mlp * on_ref[...] * summed).astype(jnp.bfloat16).astype(jnp.float32)
+            summed = last_chip[j] + last_from_chip[j]
+            cols = pl.ds(pl.multiple_of((2 * j + core) * last, last), last)
+            place = (pl.ds(pl.multiple_of(row * mine, mine), mine), cols)
+            final[place] = (h3_ref[:, cols] + scale_mlp * summed).astype(jnp.bfloat16).astype(jnp.float32)
             piece = final.at[place]
             far.append(remote(piece, piece, far_sems, (0, j), other_row))
             far[j].start()
             near.append(remote(piece, piece, far_sems, (1, j), other_core))
             near[j].start()
-        for j in range(CHUNKS):
+        for j in range(LAST_CHUNKS):
             far[j].wait_recv()
-            place = (pl.ds(pl.multiple_of((1 - row) * mine, mine), mine), pl.ds(pl.multiple_of((2 * j + core) * chunk, chunk), chunk))
+            place = (pl.ds(pl.multiple_of((1 - row) * mine, mine), mine), pl.ds(pl.multiple_of((2 * j + core) * last, last), last))
             piece = final.at[place]
             relay.append(remote(piece, piece, far_sems, (2, j), other_core))
             relay[j].start()
-        for j in range(CHUNKS):
+        for j in range(LAST_CHUNKS):
             near[j].wait_recv()
-        for j in range(CHUNKS):
+        for j in range(LAST_CHUNKS):
             relay[j].wait_recv()
         for copy in pending + near + far + relay:
             copy.wait_send()
 
     bf16, f32 = jnp.bfloat16, jnp.float32
-    chunk_shape = (2, CHUNKS, mine, chunk)
+    chunk_shape, last_shape = (CHUNKS, mine, chunk), (LAST_CHUNKS, mine, last)
     return pl.pallas_call(
         kernel,
         out_shape=jax.ShapeDtypeStruct((2 * mine, width), f32),
-        in_specs=[SMEM, SMEM] + [VMEM] * 2 + [ANY] * 5,
+        in_specs=[ANY] * 2 + [VMEM] * 2 + [ANY] * 5,
         out_specs=VMEM,
-        scratch_shapes=[pltpu.VMEM(gain.shape, bf16), pltpu.VMEM(wo.shape, bf16), pltpu.VMEM(wg.shape, bf16), pltpu.VMEM(wu.shape, bf16), pltpu.VMEM(wd.shape, bf16),
-                        pltpu.VMEM((mine, chunk), f32), pltpu.VMEM((2 * CHUNKS, mine, chunk), f32)]
+        scratch_shapes=[pltpu.SMEM(tile_rows.shape, tile_rows.dtype), pltpu.SMEM(gates.shape, gates.dtype), pltpu.VMEM(gain.shape, bf16), pltpu.VMEM(wo.shape, bf16), pltpu.VMEM(wg.shape, bf16), pltpu.VMEM(wu.shape, bf16), pltpu.VMEM(wd.shape, bf16),
+                        pltpu.VMEM((mine, LANES), f32), pltpu.VMEM((mine, width), f32)]
                        + [pltpu.VMEM((group + 1, mine, feat), f32)]
-                       + [pltpu.VMEM((mine, group * feat), bf16), pltpu.VMEM((mine, width), bf16), pltpu.VMEM((mine, ff), bf16)]
-                       + [pltpu.VMEM((2, CHUNKS, 2, mine, chunk), f32)] + [pltpu.VMEM(chunk_shape, f32)] * 3 + [pltpu.VMEM((CHUNKS, 2, mine, chunk), f32)]
-                       + [pltpu.SemaphoreType.DMA, pltpu.SemaphoreType.DMA((3,)), pltpu.SemaphoreType.DMA((2 * group,)),
-                          pltpu.SemaphoreType.DMA((2, 2, 3, CHUNKS)), pltpu.SemaphoreType.DMA((2, 1)), pltpu.SemaphoreType.DMA((2, 3, CHUNKS))],
+                       + [pltpu.VMEM((mine, group * feat), bf16), pltpu.VMEM((1, width), f32), pltpu.VMEM((mine, LANES), f32),
+                          pltpu.VMEM((mine, ff), f32), pltpu.VMEM((mine, ff), f32), pltpu.VMEM((mine, ff), bf16)]
+                       + [pltpu.VMEM((CHUNKS, 2, mine, chunk), f32)] + [pltpu.VMEM(chunk_shape, f32)] * 3 + [pltpu.VMEM((CHUNKS, 2, mine, chunk), f32)]
+                       + [pltpu.VMEM((LAST_CHUNKS, 2, mine, last), f32)] + [pltpu.VMEM(last_shape, f32)] * 3
+                       + [pltpu.SemaphoreType.DMA((3,)), pltpu.SemaphoreType.DMA((3,)), pltpu.SemaphoreType.DMA((2 * group,)),
+                          pltpu.SemaphoreType.DMA((2, 3, CHUNKS)), pltpu.SemaphoreType.DMA((2, 2, LAST_CHUNKS)), pltpu.SemaphoreType.DMA((2, 1)), pltpu.SemaphoreType.DMA((2, 3, LAST_CHUNKS))],
         compiler_params=pltpu.CompilerParams(vmem_limit_bytes=36 * 1024 * 1024, collective_id=2, has_side_effects=True),
         cost_estimate=pl.CostEstimate(flops=4 * mine * width * 3 * ff, bytes_accessed=30 * 1024 * 1024, transcendentals=mine * ff),
         name='cross_tail',
-    )(tile_rows, gates, packed, hidden_in, *in_hbm(gain, wo, wg, wu, wd))
+    )(*in_hbm(tile_rows, gates), packed, hidden_in, *in_hbm(gain, wo, wg, wu, wd))
 
 
 def cross_attention(query_bd, keys, values, tile_rows, key_new, val_new):
@@ -500,8 +535,8 @@
     width = tokens - base_one
     width_zero = min(width, -(-tile_tok // LANES) * LANES)
 
-    def kernel(tile_ref, q_ref, kin_ref, vin_ref, k_hbm, v_hbm, p_ref, kn_ref, vn_ref,
-               list_ref, o_ref, m_ref, l_ref, s_ref, kbuf, vbuf, ksem, vsem):
+    def kernel(tile_hbm, q_ref, kin_ref, vin_ref, k_hbm, v_hbm, p_ref, kn_ref, vn_ref,
+               tile_ref, list_ref, o_ref, m_ref, l_ref, s_ref, kbuf, vbuf, tsem, ksem, vsem):
         kv_index = lax.axis_index('kv')
         first_tile = kv_index * (tiles // 2)
 
@@ -538,6 +573,9 @@
                 for copy in copies(index, True, *side):
                     copy.wait()
 
+        tile_copy = pltpu.make_async_copy(tile_hbm, tile_ref, tsem)
+        tile_copy.start()
+        tile_copy.wait()
         n_zero = collect(0, jnp.int32(0))
         pairs_zero = (n_zero + 1) // 2
         for index in range(SLOTS - 1):
@@ -618,17 +656,17 @@
     return pl.pallas_call(
         kernel,
         out_shape=(jax.ShapeDtypeStruct((2, 5, half_rows, feat), jnp.float32), heads, heads),
-        in_specs=[SMEM, VMEM, VMEM, VMEM, ANY, ANY],
+        in_specs=[ANY, VMEM, VMEM, VMEM, ANY, ANY],
         out_specs=(VMEM,) * 3,
-        scratch_shapes=[pltpu.SMEM((2 * rows + 8,), jnp.int32), state, state, state,
+        scratch_shapes=[pltpu.SMEM(tile_rows.shape, jnp.int32), pltpu.SMEM((2 * rows + 8,), jnp.int32), state, state, state,
                         pltpu.VMEM((2, 16, width), jnp.float32),
                         pltpu.VMEM((SLOTS, 2 * feat, width), jnp.bfloat16),
                         pltpu.VMEM((SLOTS, 2 * feat, width), jnp.bfloat16),
-                        pltpu.SemaphoreType.DMA((SLOTS, 2)), pltpu.SemaphoreType.DMA((SLOTS, 2))],
-        compiler_params=pltpu.CompilerParams(vmem_limit_bytes=24 * 1024 * 1024),
+                        pltpu.SemaphoreType.DMA, pltpu.SemaphoreType.DMA((SLOTS, 2)), pltpu.SemaphoreType.DMA((SLOTS, 2))],
+        compiler_params=pltpu.CompilerParams(vmem_limit_bytes=30 * 1024 * 1024),
         cost_estimate=pl.CostEstimate(flops=4 * 8 * feat * tokens * rows, bytes_accessed=2 * feat * tokens * rows, transcendentals=8 * tokens * rows),
         name='cross_attention',
-    )(tile_rows, query_bd.reshape(rows * 8, feat), key_new, val_new, *in_hbm(keys, values))
+    )(*in_hbm(tile_rows), query_bd.reshape(rows * 8, feat), key_new, val_new, *in_hbm(keys, values))
 
 
 def solution(mesh):
@@ -649,7 +687,7 @@
         feat = kv_local * head_dim
         group = wq_self.shape[1] // feat
         tokens = kx_cache.shape[2]
-        freqs = jnp.tile(rope_freqs(head_dim), 2 * feat // head_dim)[None]
+        freqs = jnp.asarray(np.tile(rope_freqs(head_dim), 2 * feat // head_dim)[None])
 
         def lane_rows(gain):
             return gain.reshape(-1, LANES)

time: 92.1 us -> 84.5 us (0.917); the launches traced: 92.3 us -> 85.8 us
  Pallas kernels: 88.9 us -> 84.4 us
  local copies, waits for them, and re-layouts: 1.92 us -> 0 us
    pallas_call x1, Pallas kernels: 28.5 us -> 24.1 us  [cross_tail(): pl.pallas_call(kernel, out_shape=jax.ShapeDtypeStruct((2 * mine, width),...]
    pallas_call x1, Pallas kernels: 37.7 us -> 36.1 us  [self_layer(): pl.pallas_call(kernel, out_shape=(jax.ShapeDtypeStruct((batch, feat), f32...]
    pallas_call x1, Pallas kernels: 22.7 us -> 24.1 us  [cross_attention(): pl.pallas_call(kernel, out_shape=(jax.ShapeDtypeStruct((2, 5, half_rows,...]
    another operation x2 -> x0, local copies, waits for them, and re-layouts: 1.26 us -> none  [device_step(): freqs = jnp.tile(rope_freqs(head_dim), 2 * feat // head_dim)[None]]
where the time goes in v2:
time: 84.5 us; the launch traced here: 85.8 us
  Pallas kernels  84.4 us (100%)
    pallas_call x1, Pallas kernels, self_layer(): pl.pallas_call(kernel, out_shape=(jax.ShapeDtypeStruct((batch, feat), f32...  36.1 us
    pallas_call x1, Pallas kernels, cross_attention(): pl.pallas_call(kernel, out_shape=(jax.ShapeDtypeStruct((2, 5, half_rows,...  24.1 us
    pallas_call x1, Pallas kernels, cross_tail(): pl.pallas_call(kernel, out_shape=jax.ShapeDtypeStruct((2 * mine, width),...  24.1 us

profile of v2, /device:TPU:0, one launch (start us, length us, event | category | flops | bytes accessed | tf_op | source)
XLA Modules:
  0.0 85.8 jit_solution(5084572112203431088)
XLA Ops:
  0.6 36.1 %self_layer.1 = (f32[64,128]{1,0:T(8,128)S(1)}, f32[64,128]{1,0:T(8,128)S(1)}, f32[2,256,128]{2,1,0:T(8,128)S(1)}, f32[32,2048]{1,0:T(8,128)S(1)}) custom-call(s32[64]{0:T(128)} %seq_hbm.1, bf16[64,2048]{1,0:T(8,128)(2,1)} %x_hbm.1, bf16[16,128]{1,0:T(8,128)(2,1)} %bitcast.26, bf16[16,128]{1,0:T(8,128)(2,1)} %bitcast.27, bf16[16,128]{1,0:T(8,128)(2,1)} %bitcast.28, ...), custom_call_target="tpu_custom_call" | custom-call | flops 2013265920 | bytes 52428800 | tf_op jit(solution)/shard_map/self_layer/pallas_call | solution.py:401
  36.7 24.1 %cross_attention.1 = (f32[2,5,32,128]{3,2,1,0:T(8,128)S(1)}, bf16[64,2,64]{2,1,0:T(2,128)(2,1)}, bf16[64,2,64]{2,1,0:T(2,128)(2,1)}) custom-call(s32[4,64]{1,0:T(4,128)} %bitcast.24, f32[512,128]{1,0:T(8,128)S(1)} %bitcast.19, f32[64,128]{1,0:T(8,128)S(1)} %get-tuple-element.11.kin_ref, f32[64,128]{1,0:T(8,128)S(1)} %get-tuple-element.12.vin_ref, ...), custom_call_target="tpu_custom_call" | custom-call | flops 839385088 | bytes 52461568 | tf_op jit(solution)/shard_map/cross_attention/pallas_call | solution.py:656
  60.9 24.1 %cross_tail.1 = f32[64,2048]{1,0:T(8,128)S(1)} custom-call(s32[4,64]{1,0:T(4,128)} %bitcast.25, f32[2]{0:T(128)} %gate_hbm.1, f32[2,5,32,128]{3,2,1,0:T(8,128)S(1)} %get-tuple-element.13.p_ref, f32[32,2048]{1,0:T(8,128)S(1)} %get-tuple-element.14.h_ref, bf16[16,128]{1,0:T(8,128)(2,1)} %bitcast.29, bf16[512,2048]{1,0:T(8,128)(2,1)} %wo_hbm.3, ...), custom_call_target="tpu_custom_call" | custom-call | flops 1610612736 | bytes 31457280 | tf_op jit(solution)/shard_map/cross_tail/pallas_call | solution.py:508
  85.0 0.7 convert_element_type.3
